TPU v7x, 32 devices: a 4x4x1 block of a 4x4x8 slice. The times are simulated.
32 devices in a mesh: data: 1 (over z), dap: 32 (over y, x, core).
Axes of the slice: x: 4, y: 4, z: 1, core: 2. Of those that a mesh axis runs over, the one named last changes fastest.
The devices are a block of a 4x4x8 slice.
Arguments:
- z_one: bfloat16 [768, 768, 128], P(('data', 'dap'))
- mask_one: int32 [768, 768], P(('data', 'dap'))
- z_two: bfloat16 [768, 768, 128], P(('data', 'dap'))
- mask_two: int32 [768, 768], P(('data', 'dap'))
- norm_in: bfloat16 [2, 2, 128], replicated
- w_proj: bfloat16 [2, 128, 512], replicated
- w_gate: bfloat16 [2, 128, 128], replicated
- norm_mid: bfloat16 [2, 2, 128], replicated
- w_out: bfloat16 [2, 128, 128], replicated
Outputs:
- output 1: bfloat16 [768, 768, 128], P(('data', 'dap'))
- output 2: bfloat16 [768, 768, 128], P(('data', 'dap'))
All inputs are finite; a program needn't handle non-finite values.
Results may differ from a plain program's by a relative error of at most 0.00449604.
Values are sent between devices in bfloat16 or wider.
A program may use at most 768 MiB of HBM per device.

v0:
```python
import jax
import jax.numpy as jnp
from jax import lax
from jax.sharding import PartitionSpec as P


def layer_norm(vals, ln_gain, ln_shift, feature_axis):
    vals = vals.astype(jnp.float32)
    row_mean = jnp.mean(vals, axis=feature_axis, keepdims=True)
    centred = vals - row_mean
    row_var = jnp.mean(centred * centred, axis=feature_axis, keepdims=True)
    return centred * lax.rsqrt(row_var + 1e-5) * ln_gain.astype(jnp.float32) + ln_shift.astype(jnp.float32)


def project_rows(z_rows, mask_rows, norm_in, w_proj):
    pair_width = z_rows.shape[2]
    hidden = w_proj.shape[1] // 4
    x_norm = layer_norm(z_rows, norm_in[0], norm_in[1], -1).astype(jnp.bfloat16)
    w_split = w_proj.reshape(pair_width, 2, 2, hidden)
    projected = jnp.einsum("rnz,zsgc->sgcrn", x_norm, w_split, preferred_element_type=jnp.float32)
    keep_mask = mask_rows.astype(jnp.float32)
    sides = (keep_mask * jax.nn.sigmoid(projected[:, 1]) * projected[:, 0]).astype(jnp.bfloat16)
    return x_norm, sides


def finish_rows(z_rows, x_norm, t_rows, w_gate, norm_mid, w_out):
    t_norm = layer_norm(t_rows, norm_mid[0][:, None, None], norm_mid[1][:, None, None], 0).astype(jnp.bfloat16)
    update = jnp.einsum("crn,cz->rnz", t_norm, w_out, preferred_element_type=jnp.float32)
    gate_val = jax.nn.sigmoid(jnp.einsum("rnz,zy->rny", x_norm, w_gate, preferred_element_type=jnp.float32))
    return (z_rows.astype(jnp.float32) + gate_val * update).astype(jnp.bfloat16)


def tri_update(z_rows, mask_rows, norm_in, w_proj, w_gate, norm_mid, w_out, form):
    x_norm, sides = project_rows(z_rows, mask_rows, norm_in, w_proj)
    sides_chan = lax.all_to_all(sides, "dap", 1, 2, tiled=True)
    tri_prod = jnp.einsum(form, sides_chan[0], sides_chan[1], preferred_element_type=jnp.float32).astype(jnp.bfloat16)
    t_rows = lax.all_to_all(tri_prod, "dap", 1, 0, tiled=True)
    return finish_rows(z_rows, x_norm, t_rows, w_gate, norm_mid, w_out)


def solution(mesh):
    row_spec = P(("data", "dap"), None, None)
    mask_spec = P(("data", "dap"), None)
    replicated = P()

    def crop_update(z_rows, mask_rows, norm_in, w_proj, w_gate, norm_mid, w_out):
        z_mid = tri_update(z_rows, mask_rows, norm_in[0], w_proj[0], w_gate[0], norm_mid[0], w_out[0], "cik,cjk->cij")
        return tri_update(z_mid, mask_rows, norm_in[1], w_proj[1], w_gate[1], norm_mid[1], w_out[1], "cki,ckj->cij")

    def per_device(z_one, mask_one, z_two, mask_two, norm_in, w_proj, w_gate, norm_mid, w_out):
        return (crop_update(z_one, mask_one, norm_in, w_proj, w_gate, norm_mid, w_out),
                crop_update(z_two, mask_two, norm_in, w_proj, w_gate, norm_mid, w_out))

    return jax.shard_map(per_device, mesh=mesh,
                         in_specs=(row_spec, mask_spec, row_spec, mask_spec, replicated, replicated, replicated, replicated, replicated),
                         out_specs=(row_spec, row_spec), check_vma=False)
```

profile of v0, /device:TPU:97, one launch (start us, length us, event | category | flops | bytes accessed | tf_op | source)
XLA Modules:
  0.0 1018.1 jit_solution(18155754673495966250)
XLA Ops:
  0.7 6.7 copy.153
  15.6 17.4 %convolution_bitcast_fusion.3 = f32[2,2,128,24,768]{2,4,1,0,3:T(8,128)} fusion(bf16[128,2,2,128,1]{0,3,2,1,4:T(8,128)(2,1)S(1)} %bitcast.289, bf16[24,768,128]{1,2,0:T(8,128)(2,1)} %copy.153, f32[128]{0:T(128)S(1)} %get-tuple-element.29, f32[128]{0:T(128)S(1)} %get-tuple-element.30, f32[24,768]{1,0:T(8,128)S(1)} %add_rsqrt_fusion.7, ...), kind=kOutput, calls=%fused_computation.52 | convolution fusion | flops 2430074880 | bytes 42746880 | tf_op jit(solution)/shard_map/rnz,zsgc->sgcrn/dot_general | solution.py:20
  33.0 16.7 %fusion.22 = bf16[2,128,24,768]{1,3,0,2:T(8,128)(2,1)} fusion(f32[2,2,128,24,768]{2,4,1,0,3:T(8,128)} %convolution_bitcast_fusion.3, f32[24,768]{1,0:T(8,128)S(1)} %convert_element_type.206), kind=kLoop, calls=%fused_computation.29 | loop fusion | flops 28311552 | bytes 47259648 | tf_op jit(solution)/shard_map/convert_element_type | solution.py:22
  49.7 23.9 %copy.160 = bf16[2,128,24,768]{3,0,2,1:T(2,128)(2,1)} copy(bf16[2,128,24,768]{1,3,0,2:T(8,128)(2,1)} %fusion.22) | data formatting | bytes 18874368 | tf_op jit(solution)/shard_map/convert_element_type | solution.py:22
  73.6 10.1 all-to-all-start
  83.7 6.6 copy.185
  97.4 14.8 %convolution_bitcast_fusion.1 = f32[2,2,128,24,768]{2,4,0,3,1:T(8,128)} fusion(bf16[128,2,2,128,1]{0,3,2,1,4:T(8,128)(2,1)S(1)} %bitcast.290, bf16[24,768,128]{1,2,0:T(8,128)(2,1)S(1)} %copy-done, f32[24,768]{1,0:T(8,128)S(1)} %add_rsqrt_fusion.3, f32[24,768]{1,0:T(8,128)S(1)} %broadcast_multiply_fusion.3, f32[128]{0:T(128)S(1)} %get-tuple-element.29, ...), kind=kOutput, calls=%fused_computation.38 | convolution fusion | flops 2430074880 | bytes 42746880 | tf_op jit(solution)/shard_map/rnz,zsgc->sgcrn/dot_general | solution.py:20
  112.3 16.7 %fusion.8 = bf16[2,128,24,768]{1,3,0,2:T(8,128)(2,1)} fusion(f32[2,2,128,24,768]{2,4,0,3,1:T(8,128)} %convolution_bitcast_fusion.1, f32[24,768]{1,0:T(8,128)S(1)} %convert_element_type.235), kind=kLoop, calls=%fused_computation.11 | loop fusion | flops 28311552 | bytes 47259648 | tf_op jit(solution)/shard_map/convert_element_type | solution.py:22
  129.0 23.9 %copy.190 = bf16[2,128,24,768]{3,0,2,1:T(2,128)(2,1)} copy(bf16[2,128,24,768]{1,3,0,2:T(8,128)(2,1)} %fusion.8) | data formatting | bytes 18874368 | tf_op jit(solution)/shard_map/convert_element_type | solution.py:22
  152.9 49.0 %all-to-all-done = bf16[2,128,24,768]{3,0,2,1:T(2,128)(2,1)} async-done(((bf16[2,128,24,768]{3,0,2,1:T(2,128)(2,1)}), bf16[2,128,24,768]{3,0,2,1:T(2,128)(2,1)}, u32[]{:S(2)}, u32[]{:S(2)}) %all-to-all-start) | async-done | bytes 9437216 | tf_op jit(solution)/shard_map/all_to_all | solution.py:35
  201.9 14.1 %all-to-all-start.4 = ((bf16[2,128,24,768]{3,0,2,1:T(2,128)(2,1)}), bf16[2,128,24,768]{3,0,2,1:T(2,128)(2,1)}, u32[]{:S(2)}, u32[]{:S(2)}) async-start(bf16[2,128,24,768]{3,0,2,1:T(2,128)(2,1)} %copy.190), calls=%async_computation.4 | async-start | bytes 18874368 | tf_op jit(solution)/shard_map/all_to_all | solution.py:35
  216.0 8.6 copy.161
  233.8 5.9 copy.164
  239.6 93.1 %all-to-all-done.4 = bf16[2,128,24,768]{3,0,2,1:T(2,128)(2,1)} async-done(((bf16[2,128,24,768]{3,0,2,1:T(2,128)(2,1)}), bf16[2,128,24,768]{3,0,2,1:T(2,128)(2,1)}, u32[]{:S(2)}, u32[]{:S(2)}) %all-to-all-start.4) | async-done | bytes 9437216 | tf_op jit(solution)/shard_map/all_to_all | solution.py:35
  332.8 15.6 %all-to-all-start.1 = ((bf16[4,768,768]{2,0,1:T(4,128)(2,1)}), bf16[4,768,768]{2,0,1:T(4,128)(2,1)}, u32[]{:S(2)}, u32[]{:S(2)}) async-start(bf16[4,768,768]{2,0,1:T(4,128)(2,1)} %copy.164), calls=%async_computation.1 | async-start | bytes 9437184 | tf_op jit(solution)/shard_map/all_to_all | solution.py:37
  348.4 8.5 copy.191
  371.9 34.3 %all-to-all-done.1 = bf16[4,768,768]{2,0,1:T(4,128)(2,1)} async-done(((bf16[4,768,768]{2,0,1:T(4,128)(2,1)}), bf16[4,768,768]{2,0,1:T(4,128)(2,1)}, u32[]{:S(2)}, u32[]{:S(2)}) %all-to-all-start.1) | async-done | bytes 4718624 | tf_op jit(solution)/shard_map/all_to_all | solution.py:37
  406.2 9.1 all-to-all-start.5
  416.3 8.2 fusion.104
  434.5 38.3 %all-to-all-done.5 = bf16[4,768,768]{2,0,1:T(4,128)(2,1)} async-done(((bf16[4,768,768]{2,0,1:T(4,128)(2,1)}), bf16[4,768,768]{2,0,1:T(4,128)(2,1)}, u32[]{:S(2)}, u32[]{:S(2)}) %all-to-all-start.5) | async-done | bytes 4718624 | tf_op jit(solution)/shard_map/all_to_all | solution.py:37
  483.0 10.9 %fusion.72 = (bf16[32,4,24,768]{3,1,2,0:T(4,128)(2,1)}, bf16[32,4,24,768]{3,1,2,0:T(4,128)(2,1)S(1)}) fusion(bf16[4,32,24,768]{3,0,2,1:T(4,128)(2,1)} %bitcast.53, f32[24,768]{1,0:T(8,128)S(1)} %add_rsqrt_fusion.2, f32[24,768]{1,0:T(8,128)S(1)} %broadcast_multiply_fusion.2, f32[32,4]{1,0:T(8,128)S(1)} %reshape.225, f32[32,4]{1,0:T(8,128)S(1)} %reshape.224, ...), kind=kLoop, calls=%fused_computation.98 | loop fusion | flops 28311552 | bytes 19170304 | tf_op jit(solution)/shard_map/convert_element_type | solution.py:27
  498.5 8.5 convert_element_type.217
  507.0 10.0 convert_reduce_fusion.2
  518.5 14.8 %convolution_bitcast_fusion.2 = f32[2,2,128,24,768]{2,4,0,3,1:T(8,128)} fusion(bf16[128,2,2,128,1]{0,3,2,1,4:T(8,128)(2,1)S(1)} %bitcast.287, bf16[24,768,128]{1,2,0:T(8,128)(2,1)S(1)} %get-tuple-element.35, f32[128]{0:T(128)S(1)} %copy-done.23, f32[128]{0:T(128)S(1)} %copy-done.22, f32[24,768]{1,0:T(8,128)S(1)} %add_rsqrt_fusion.5, ...), kind=kOutput, calls=%fused_computation.39 | convolution fusion | flops 2430074880 | bytes 42746880 | tf_op jit(solution)/shard_map/rnz,zsgc->sgcrn/dot_general | solution.py:20
  533.4 16.7 %fusion.15 = bf16[2,128,24,768]{1,3,0,2:T(8,128)(2,1)} fusion(f32[2,2,128,24,768]{2,4,0,3,1:T(8,128)} %convolution_bitcast_fusion.2, f32[24,768]{1,0:T(8,128)S(1)} %copy-done.15), kind=kLoop, calls=%fused_computation.20 | loop fusion | flops 28311552 | bytes 47259648 | tf_op jit(solution)/shard_map/convert_element_type | solution.py:22
  550.1 23.9 %copy.173 = bf16[2,128,24,768]{3,0,2,1:T(2,128)(2,1)} copy(bf16[2,128,24,768]{1,3,0,2:T(8,128)(2,1)} %fusion.15) | data formatting | bytes 18874368 | tf_op jit(solution)/shard_map/convert_element_type | solution.py:22
  574.0 9.6 all-to-all-start.2
  583.7 8.2 fusion.102
  591.8 6.9 copy.195
  598.8 8.5 convert_element_type.242
  607.3 10.1 convert_reduce_fusion
  618.8 14.8 %convolution_bitcast_fusion = f32[2,2,128,24,768]{2,4,0,3,1:T(8,128)} fusion(bf16[128,2,2,128,1]{0,3,2,1,4:T(8,128)(2,1)S(1)} %bitcast.288, bf16[24,768,128]{1,2,0:T(8,128)(2,1)S(1)} %get-tuple-element.33, f32[24,768]{1,0:T(8,128)S(1)} %add_rsqrt_fusion.1, f32[24,768]{1,0:T(8,128)S(1)} %broadcast_multiply_fusion.1, f32[128]{0:T(128)S(1)} %copy-done.23, ...), kind=kOutput, calls=%fused_computation.37 | convolution fusion | flops 2430074880 | bytes 42746880 | tf_op jit(solution)/shard_map/rnz,zsgc->sgcrn/dot_general | solution.py:20
  633.7 16.9 %fusion.1 = bf16[2,128,24,768]{1,3,0,2:T(8,128)(2,1)} fusion(f32[2,2,128,24,768]{2,4,0,3,1:T(8,128)} %convolution_bitcast_fusion, f32[24,768]{1,0:T(8,128)S(1)} %copy-done.13), kind=kLoop, calls=%fused_computation.2 | loop fusion | flops 28311552 | bytes 47259648 | tf_op jit(solution)/shard_map/convert_element_type | solution.py:22
  650.6 23.9 %copy.201 = bf16[2,128,24,768]{3,0,2,1:T(2,128)(2,1)} copy(bf16[2,128,24,768]{1,3,0,2:T(8,128)(2,1)} %fusion.1) | data formatting | bytes 18874368 | tf_op jit(solution)/shard_map/convert_element_type | solution.py:22
  674.5 24.6 %all-to-all-done.2 = bf16[2,128,24,768]{3,0,2,1:T(2,128)(2,1)} async-done(((bf16[2,128,24,768]{3,0,2,1:T(2,128)(2,1)}), bf16[2,128,24,768]{3,0,2,1:T(2,128)(2,1)}, u32[]{:S(2)}, u32[]{:S(2)}) %all-to-all-start.2) | async-done | bytes 9437216 | tf_op jit(solution)/shard_map/all_to_all | solution.py:35
  699.1 16.3 %all-to-all-start.6 = ((bf16[2,128,24,768]{3,0,2,1:T(2,128)(2,1)}), bf16[2,128,24,768]{3,0,2,1:T(2,128)(2,1)}, u32[]{:S(2)}, u32[]{:S(2)}) async-start(bf16[2,128,24,768]{3,0,2,1:T(2,128)(2,1)} %copy.201), calls=%async_computation.6 | async-start | bytes 18874368 | tf_op jit(solution)/shard_map/all_to_all | solution.py:35
  715.4 8.6 copy.174
  739.1 91.8 %all-to-all-done.6 = bf16[2,128,24,768]{3,0,2,1:T(2,128)(2,1)} async-done(((bf16[2,128,24,768]{3,0,2,1:T(2,128)(2,1)}), bf16[2,128,24,768]{3,0,2,1:T(2,128)(2,1)}, u32[]{:S(2)}, u32[]{:S(2)}) %all-to-all-start.6) | async-done | bytes 9437216 | tf_op jit(solution)/shard_map/all_to_all | solution.py:35
  831.0 16.5 %all-to-all-start.3 = ((bf16[4,768,768]{2,0,1:T(4,128)(2,1)}), bf16[4,768,768]{2,0,1:T(4,128)(2,1)}, u32[]{:S(2)}, u32[]{:S(2)}) async-start(bf16[4,768,768]{2,0,1:T(4,128)(2,1)} %copy.178), calls=%async_computation.3 | async-start | bytes 9437184 | tf_op jit(solution)/shard_map/all_to_all | solution.py:37
  847.5 8.5 copy.202
  871.2 34.0 %all-to-all-done.3 = bf16[4,768,768]{2,0,1:T(4,128)(2,1)} async-done(((bf16[4,768,768]{2,0,1:T(4,128)(2,1)}), bf16[4,768,768]{2,0,1:T(4,128)(2,1)}, u32[]{:S(2)}, u32[]{:S(2)}) %all-to-all-start.3) | async-done | bytes 4718624 | tf_op jit(solution)/shard_map/all_to_all | solution.py:37
  905.3 9.4 all-to-all-start.7
  921.5 51.4 %all-to-all-done.7 = bf16[4,768,768]{2,0,1:T(4,128)(2,1)} async-done(((bf16[4,768,768]{2,0,1:T(4,128)(2,1)}), bf16[4,768,768]{2,0,1:T(4,128)(2,1)}, u32[]{:S(2)}, u32[]{:S(2)}) %all-to-all-start.7) | async-done | bytes 4718624 | tf_op jit(solution)/shard_map/all_to_all | solution.py:37
  978.1 6.0 fusion.64
  986.5 6.5 fusion.56
  993.0 6.9 copy.212
  1004.5 6.5 fusion.54
  1011.0 6.6 copy.211
  (140 shorter events, 116.8 us)
Async XLA Ops:
  0.6 13.5 %copy-start.24 = (bf16[2,2,128]{2,1,0:T(2,128)(2,1)S(1)}, bf16[2,2,128]{2,1,0:T(2,128)(2,1)}, u32[]{:S(2)}) copy-start(bf16[2,2,128]{2,1,0:T(2,128)(2,1)} %param.13) | copy-start | bytes 3076
  0.6 14.1 %copy-start.17 = (bf16[2,128,512]{2,1,0:T(8,128)(2,1)S(1)}, bf16[2,128,512]{2,1,0:T(8,128)(2,1)}, u32[]{:S(2)}) copy-start(bf16[2,128,512]{2,1,0:T(8,128)(2,1)} %param.14) | copy-start | bytes 786436
  0.7 14.9 %copy-start.18 = (s32[24,768]{1,0:T(8,128)S(1)}, s32[24,768]{1,0:T(8,128)}, u32[]{:S(2)}) copy-start(s32[24,768]{1,0:T(8,128)} %param.10) | copy-start | bytes 221188
  15.6 17.4 %copy-start.14 = (f32[24,768]{1,0:T(8,128)}, f32[24,768]{1,0:T(8,128)S(1)}, u32[]{:S(2)}) copy-start(f32[24,768]{1,0:T(8,128)S(1)} %convert_element_type.206) | copy-start | bytes 221188
  73.6 128.3 %all-to-all-start = ((bf16[2,128,24,768]{3,0,2,1:T(2,128)(2,1)}), bf16[2,128,24,768]{3,0,2,1:T(2,128)(2,1)}, u32[]{:S(2)}, u32[]{:S(2)}) async-start(bf16[2,128,24,768]{3,0,2,1:T(2,128)(2,1)} %copy.160), calls=%async_computation | async-start | bytes 18874368 | tf_op jit(solution)/shard_map/all_to_all | solution.py:35
  83.7 6.7 copy-start.19
  90.4 7.0 copy-start
  90.4 21.9 %copy-start.12 = (f32[24,768]{1,0:T(8,128)}, f32[24,768]{1,0:T(8,128)S(1)}, u32[]{:S(2)}) copy-start(f32[24,768]{1,0:T(8,128)S(1)} %convert_element_type.235) | copy-start | bytes 221188
  93.6 18.6 %copy-start.4 = (f32[24,768]{1,0:T(8,128)}, f32[24,768]{1,0:T(8,128)S(1)}, u32[]{:S(2)}) copy-start(f32[24,768]{1,0:T(8,128)S(1)} %broadcast_multiply_fusion.3) | copy-start | bytes 221188
  97.4 14.8 %copy-start.6 = (f32[24,768]{1,0:T(8,128)}, f32[24,768]{1,0:T(8,128)S(1)}, u32[]{:S(2)}) copy-start(f32[24,768]{1,0:T(8,128)S(1)} %add_rsqrt_fusion.3) | copy-start | bytes 221188
  201.9 130.9 %all-to-all-start.4 = ((bf16[2,128,24,768]{3,0,2,1:T(2,128)(2,1)}), bf16[2,128,24,768]{3,0,2,1:T(2,128)(2,1)}, u32[]{:S(2)}, u32[]{:S(2)}) async-start(bf16[2,128,24,768]{3,0,2,1:T(2,128)(2,1)} %copy.190), calls=%async_computation.4 | async-start | bytes 18874368 | tf_op jit(solution)/shard_map/all_to_all | solution.py:35
  332.8 73.4 %all-to-all-start.1 = ((bf16[4,768,768]{2,0,1:T(4,128)(2,1)}), bf16[4,768,768]{2,0,1:T(4,128)(2,1)}, u32[]{:S(2)}, u32[]{:S(2)}) async-start(bf16[4,768,768]{2,0,1:T(4,128)(2,1)} %copy.164), calls=%async_computation.1 | async-start | bytes 9437184 | tf_op jit(solution)/shard_map/all_to_all | solution.py:37
  366.1 49.2 %copy-start.25 = (bf16[2,2,128]{2,1,0:T(2,128)(2,1)S(1)}, bf16[2,2,128]{2,1,0:T(2,128)(2,1)}, u32[]{:S(2)}) copy-start(bf16[2,2,128]{2,1,0:T(2,128)(2,1)} %param.16) | copy-start | bytes 3076
  366.1 50.0 %copy-start.16 = (bf16[1,128,512]{2,1,0:T(8,128)(2,1)S(1)}, bf16[1,128,512]{2,1,0:T(8,128)(2,1)}, u32[]{:S(2)}) copy-start(bf16[1,128,512]{2,1,0:T(8,128)(2,1)} %get-tuple-element.22) | copy-start | bytes 393220
  366.1 50.2 %copy-start.21 = (bf16[2,128,128]{2,1,0:T(8,128)(2,1)S(1)}, bf16[2,128,128]{2,1,0:T(8,128)(2,1)}, u32[]{:S(2)}) copy-start(bf16[2,128,128]{2,1,0:T(8,128)(2,1)} %param.15) | copy-start | bytes 196612
  406.2 66.6 %all-to-all-start.5 = ((bf16[4,768,768]{2,0,1:T(4,128)(2,1)}), bf16[4,768,768]{2,0,1:T(4,128)(2,1)}, u32[]{:S(2)}, u32[]{:S(2)}) async-start(bf16[4,768,768]{2,0,1:T(4,128)(2,1)} %copy.194), calls=%async_computation.5 | async-start | bytes 9437184 | tf_op jit(solution)/shard_map/all_to_all | solution.py:37
  493.9 13.1 %copy-start.20 = (bf16[2,128,128]{2,1,0:T(8,128)(2,1)S(1)}, bf16[2,128,128]{2,1,0:T(8,128)(2,1)}, u32[]{:S(2)}) copy-start(bf16[2,128,128]{2,1,0:T(8,128)(2,1)} %param.17) | copy-start | bytes 196612
  507.0 11.5 %copy-start.22 = (f32[128]{0:T(128)S(1)}, f32[128]{0:T(128)}, u32[]{:S(2)}) copy-start(f32[128]{0:T(128)} %get-tuple-element.28) | copy-start | bytes 1540
  507.0 11.5 %copy-start.23 = (f32[128]{0:T(128)S(1)}, f32[128]{0:T(128)}, u32[]{:S(2)}) copy-start(f32[128]{0:T(128)} %get-tuple-element.31) | copy-start | bytes 1540
  517.1 16.3 %copy-start.2 = (bf16[24,768,128]{1,2,0:T(8,128)(2,1)}, bf16[24,768,128]{1,2,0:T(8,128)(2,1)S(1)}, u32[]{:S(2)}) copy-start(bf16[24,768,128]{1,2,0:T(8,128)(2,1)S(1)} %get-tuple-element.35) | copy-start | bytes 14155780
  517.1 16.3 %copy-start.8 = (f32[24,768]{1,0:T(8,128)}, f32[24,768]{1,0:T(8,128)S(1)}, u32[]{:S(2)}) copy-start(f32[24,768]{1,0:T(8,128)S(1)} %broadcast_multiply_fusion.5) | copy-start | bytes 221188
  518.5 14.9 %copy-start.10 = (f32[24,768]{1,0:T(8,128)}, f32[24,768]{1,0:T(8,128)S(1)}, u32[]{:S(2)}) copy-start(f32[24,768]{1,0:T(8,128)S(1)} %add_rsqrt_fusion.5) | copy-start | bytes 221188
  518.5 14.8 %copy-start.15 = (f32[24,768]{1,0:T(8,128)S(1)}, f32[24,768]{1,0:T(8,128)}, u32[]{:S(2)}) copy-start(f32[24,768]{1,0:T(8,128)} %copy-done.14) | copy-start | bytes 221188
  574.0 9.6 copy-start.5
  574.0 9.6 copy-start.7
  574.0 125.1 %all-to-all-start.2 = ((bf16[2,128,24,768]{3,0,2,1:T(2,128)(2,1)}), bf16[2,128,24,768]{3,0,2,1:T(2,128)(2,1)}, u32[]{:S(2)}, u32[]{:S(2)}) async-start(bf16[2,128,24,768]{3,0,2,1:T(2,128)(2,1)} %copy.173), calls=%async_computation.2 | async-start | bytes 18874368 | tf_op jit(solution)/shard_map/all_to_all | solution.py:35
  617.4 16.3 %copy-start.3 = (bf16[24,768,128]{1,2,0:T(8,128)(2,1)}, bf16[24,768,128]{1,2,0:T(8,128)(2,1)S(1)}, u32[]{:S(2)}) copy-start(bf16[24,768,128]{1,2,0:T(8,128)(2,1)S(1)} %get-tuple-element.33) | copy-start | bytes 14155780
  618.8 14.8 %copy-start.13 = (f32[24,768]{1,0:T(8,128)S(1)}, f32[24,768]{1,0:T(8,128)}, u32[]{:S(2)}) copy-start(f32[24,768]{1,0:T(8,128)} %copy-done.12) | copy-start | bytes 221188
  699.1 131.9 %all-to-all-start.6 = ((bf16[2,128,24,768]{3,0,2,1:T(2,128)(2,1)}), bf16[2,128,24,768]{3,0,2,1:T(2,128)(2,1)}, u32[]{:S(2)}, u32[]{:S(2)}) async-start(bf16[2,128,24,768]{3,0,2,1:T(2,128)(2,1)} %copy.201), calls=%async_computation.6 | async-start | bytes 18874368 | tf_op jit(solution)/shard_map/all_to_all | solution.py:35
  831.0 74.3 %all-to-all-start.3 = ((bf16[4,768,768]{2,0,1:T(4,128)(2,1)}), bf16[4,768,768]{2,0,1:T(4,128)(2,1)}, u32[]{:S(2)}, u32[]{:S(2)}) async-start(bf16[4,768,768]{2,0,1:T(4,128)(2,1)} %copy.178), calls=%async_computation.3 | async-start | bytes 9437184 | tf_op jit(solution)/shard_map/all_to_all | solution.py:37
  865.4 49.3 %copy-start.27 = (f32[128]{0:T(128)S(1)}, f32[128]{0:T(128)}, u32[]{:S(2)}) copy-start(f32[128]{0:T(128)} %get-tuple-element.10) | copy-start | bytes 1540
  865.4 49.5 %copy-start.26 = (f32[128]{0:T(128)S(1)}, f32[128]{0:T(128)}, u32[]{:S(2)}) copy-start(f32[128]{0:T(128)} %get-tuple-element.13) | copy-start | bytes 1540
  905.3 67.7 %all-to-all-start.7 = ((bf16[4,768,768]{2,0,1:T(4,128)(2,1)}), bf16[4,768,768]{2,0,1:T(4,128)(2,1)}, u32[]{:S(2)}, u32[]{:S(2)}) async-start(bf16[4,768,768]{2,0,1:T(4,128)(2,1)} %copy.206), calls=%async_computation.7 | async-start | bytes 9437184 | tf_op jit(solution)/shard_map/all_to_all | solution.py:37
  918.0 2.2 copy-start.1
  921.5 56.4 %slice-start = ((s8[4718592]{0:T(1024)(128)(4,1)}), s8[524288]{0:T(1024)(128)(4,1)S(1)}, s32[]{:S(2)}) async-start(s8[4718592]{0:T(1024)(128)(4,1)} %bitcast.263), calls=%async_computation.8 | async-start | bytes 1048576
  975.9 2.2 slice-start.1
  984.1 2.2 slice-start.4
  984.7 1.8 slice-start.5
  999.9 4.6 slice-start.2
  1003.0 1.5 slice-start.3
  1003.0 1.5 copy-start.9
  1003.0 1.5 copy-start.11
where the time goes:
time: 1030 us; the launch traced here: 1020 us
  waiting for transfers between devices  417 us (40%)
  local copies, waits for them, and re-layouts  242 us (23%)
  matrix products  131 us (13%)
  other arithmetic  126 us (12%)
  starting transfers between devices  101 us (10%)
    all_to_all x4, waiting for transfers between devices, tri_update(): sides_chan = lax.all_to_all(sides, 'dap', 1, 2, tiled=True)  259 us
    all_to_all x4, waiting for transfers between devices, tri_update(): t_rows = lax.all_to_all(tri_prod, 'dap', 1, 0, tiled=True)  158 us
    convert_element_type x4, local copies, waits for them, and re-layouts, project_rows(): (keep_mask * jax.nn.sigmoid(projected[:, 1]) * projected[:, 0]).astype(jn...  95.7 us
    convert_element_type x4, other arithmetic, project_rows(): (keep_mask * jax.nn.sigmoid(projected[:, 1]) * projected[:, 0]).astype(jn...  67.1 us
    dot_general x4, matrix products, project_rows(): jnp.einsum('rnz,zsgc->sgcrn', x_norm, w_split, preferred_element_type=jnp...  61.9 us
    all_to_all x4, starting transfers between devices, tri_update(): t_rows = lax.all_to_all(tri_prod, 'dap', 1, 0, tiled=True)  50.6 us
    all_to_all x4, starting transfers between devices, tri_update(): sides_chan = lax.all_to_all(sides, 'dap', 1, 2, tiled=True)  50.1 us
    all_to_all x4, local copies, waits for them, and re-layouts, tri_update(): sides_chan = lax.all_to_all(sides, 'dap', 1, 2, tiled=True)  34.3 us
  transfers between devices with their start and end apart: 8, of which 8 were waited for; matrix products, arithmetic and copies ran while one was open for 27% of the time, Pallas kernels for 0%

commit v1 on v0

v1 whole, which is shorter than its diff:
```python
import functools

import jax
import jax.numpy as jnp
from jax import lax
from jax.experimental import pallas as pl
from jax.experimental.pallas import tpu as pltpu
from jax.sharding import PartitionSpec as P

RB = 8
LANES = 128
F32, BF16 = jnp.float32, jnp.bfloat16


def _norm_cols(v, gain, shift):
    mean = jnp.mean(v, axis=0, keepdims=True)
    cen = v - mean
    var = jnp.mean(cen * cen, axis=0, keepdims=True)
    return (cen * lax.rsqrt(var + 1e-5) * gain + shift).astype(BF16)


def _mm(a, b):
    return lax.dot_general(a, b, (((1,), (0,)), ((), ())), preferred_element_type=F32)


def _project(z_t, norm_ref, wp_ref, scr, r, kk):
    hid = wp_ref.shape[0] // 4
    x_t = _norm_cols(z_t, norm_ref[0], norm_ref[1])
    q = _mm(wp_ref[...], x_t)
    for s in range(2):
        p, g = q[2 * s * hid:(2 * s + 1) * hid], q[(2 * s + 1) * hid:(2 * s + 2) * hid]
        scr[kk, pl.ds(s * hid * RB + r, hid, stride=RB), :] = jax.nn.sigmoid(g) * p


def _emit_sides(scr, m_ref, out_ref, kk):
    n, _, cl = out_ref.shape[:3]
    half = n * cl * RB
    lanes = slice(kk * LANES, (kk + 1) * LANES)
    keep = m_ref[:, lanes].astype(F32)
    for s in range(2):
        for d in range(n):
            v = scr[kk, pl.ds(s * half + d * cl * RB, cl * RB), :].reshape(cl, RB, LANES)
            out_ref[d, s, :, :, lanes] = (v * keep).astype(BF16)


def _finish(z_t, r, kk, scr_y, norm_ref, mid_ref, wg_ref, wo_ref):
    hid = wo_ref.shape[1]
    x_t = _norm_cols(z_t, norm_ref[0], norm_ref[1])
    gate = jax.nn.sigmoid(_mm(wg_ref[...], x_t))
    y = scr_y[kk, pl.ds(r, hid, stride=RB), :]
    y = (y * mid_ref[0] + mid_ref[1]).astype(BF16)
    return (z_t + gate * _mm(wo_ref[...], y)).astype(BF16)


def _norm_mid(t_ref, scr_y, kk):
    n, cl = t_ref.shape[:2]
    lanes = slice(kk * LANES, (kk + 1) * LANES)
    tot = n * cl

    def load(i):
        return t_ref[i, :, :, lanes].astype(F32)

    zero = jnp.zeros((RB, LANES), F32)
    mean = lax.fori_loop(0, n, lambda i, a: a + jnp.sum(load(i), axis=0), zero, unroll=8) * (1.0 / tot)

    def sq(i, a):
        c = load(i) - mean
        return a + jnp.sum(c * c, axis=0)
    var = lax.fori_loop(0, n, sq, zero, unroll=8) * (1.0 / tot)
    inv = lax.rsqrt(var + 1e-5)

    def put(i, c):
        v = (load(i) - mean) * inv
        scr_y[kk, pl.ds(pl.multiple_of(i * cl * RB, cl * RB), cl * RB), :] = v.reshape(cl * RB, LANES)
        return c
    lax.fori_loop(0, n, put, 0, unroll=8)


def _row_loop(f):
    def body(r, c):
        f(r)
        return c
    lax.fori_loop(0, RB, body, 0)


def _project_kernel(z_ref, m_ref, norm_ref, wp_ref, out_ref, scr):
    for kk in range(z_ref.shape[1] // LANES):
        lanes = slice(kk * LANES, (kk + 1) * LANES)

        def row(r):
            z_t = z_ref[r, lanes, :].astype(F32).T
            _project(z_t, norm_ref, wp_ref, scr, r, kk)
        _row_loop(row)
        _emit_sides(scr, m_ref, out_ref, kk)


def _finish_project_kernel(z_ref, t_ref, m_ref, n0_ref, mid_ref, wg_ref, wo_ref, n1_ref, wp_ref, zt_ref, out_ref, scr_y, scr):
    for kk in range(z_ref.shape[1] // LANES):
        lanes = slice(kk * LANES, (kk + 1) * LANES)
        _norm_mid(t_ref, scr_y, kk)

        def row(r):
            z_t = z_ref[r, lanes, :].astype(F32).T
            z_new = _finish(z_t, r, kk, scr_y, n0_ref, mid_ref, wg_ref, wo_ref)
            zt_ref[r, :, lanes] = z_new
            _project(z_new.astype(F32), n1_ref, wp_ref, scr, r, kk)
        _row_loop(row)
        _emit_sides(scr, m_ref, out_ref, kk)


def _finish_kernel(zt_ref, t_ref, n0_ref, mid_ref, wg_ref, wo_ref, z_ref, scr_y):
    for kk in range(z_ref.shape[1] // LANES):
        lanes = slice(kk * LANES, (kk + 1) * LANES)
        _norm_mid(t_ref, scr_y, kk)

        def row(r):
            z_new = _finish(zt_ref[r, :, lanes].astype(F32), r, kk, scr_y, n0_ref, mid_ref, wg_ref, wo_ref)
            z_ref[r, lanes, :] = z_new.astype(F32).T.astype(BF16)
        _row_loop(row)


def _triangle_kernel(contract, a_ref, b_ref, out_ref):
    n, _, _, rows, width = a_ref.shape
    a = a_ref[...].reshape(n * rows, width)
    b = b_ref[...].reshape(n * rows, width)
    t = lax.dot_general(a, b, (((contract,), (contract,)), ((), ())), preferred_element_type=F32)
    out_ref[...] = t.astype(BF16).reshape(out_ref.shape)


def _whole(a):
    return pl.BlockSpec(a.shape, lambda *_: (0,) * a.ndim)


def _cost(flops, nbytes):
    return pl.CostEstimate(flops=flops, bytes_accessed=nbytes, transcendentals=0)


PARAMS = pltpu.CompilerParams(vmem_limit_bytes=60 * 1024 * 1024)


class Shapes:
    def __init__(self, n, z, w_proj):
        self.n, (self.rows, self.width, self.cz) = n, z.shape
        self.hid = w_proj.shape[-1] // 4
        self.cl = self.hid // n
        self.kb = 2 * LANES if self.width % (2 * LANES) == 0 else LANES
        self.grid = (self.rows // RB, self.width // self.kb)
        self.z_spec = pl.BlockSpec((RB, self.kb, self.cz), lambda i, j: (i, j, 0))
        self.zt_spec = pl.BlockSpec((RB, self.cz, self.kb), lambda i, j: (i, 0, j))
        self.m_spec = pl.BlockSpec((RB, self.kb), lambda i, j: (i, j))
        self.sides_spec = pl.BlockSpec((n, 2, self.cl, RB, self.kb), lambda i, j: (0, 0, 0, i, j))
        self.t_spec = pl.BlockSpec((n, self.cl, RB, self.kb), lambda i, j: (0, 0, i, j))
        self.sides = jax.ShapeDtypeStruct((n, 2, self.cl, self.rows, self.width), BF16)
        self.tri = jax.ShapeDtypeStruct((n, self.cl, self.rows, self.width), BF16)
        self.zt = jax.ShapeDtypeStruct((self.rows, self.cz, self.width), BF16)
        self.scr = pltpu.VMEM((self.kb // LANES, 2 * self.hid * RB, LANES), F32)
        self.scr_y = pltpu.VMEM((self.kb // LANES, self.hid * RB, LANES), F32)
        pos = self.rows * self.width
        self.f_proj = 2 * pos * self.cz * 4 * self.hid
        self.f_fin = 4 * pos * self.cz * self.hid
        self.f_tri = 2 * self.cl * self.width ** 3
        self.bytes = 2 * pos * self.cz * 4


def project(sh, z, m, norm, wp):
    return pl.pallas_call(
        _project_kernel, grid=sh.grid, out_shape=sh.sides,
        in_specs=[sh.z_spec, sh.m_spec, _whole(norm), _whole(wp)], out_specs=sh.sides_spec,
        scratch_shapes=[sh.scr], compiler_params=PARAMS, cost_estimate=_cost(sh.f_proj * 8, sh.bytes), name="project",
    )(z, m, norm, wp)


def finish_project(sh, z, t, m, n0, mid, wg, wo, n1, wp):
    return pl.pallas_call(
        _finish_project_kernel, grid=sh.grid, out_shape=(sh.zt, sh.sides),
        in_specs=[sh.z_spec, sh.t_spec, sh.m_spec] + [_whole(a) for a in (n0, mid, wg, wo, n1, wp)],
        out_specs=(sh.zt_spec, sh.sides_spec), scratch_shapes=[sh.scr_y, sh.scr], compiler_params=PARAMS,
        cost_estimate=_cost((sh.f_proj + sh.f_fin) * 8, 2 * sh.bytes), name="finish_project",
    )(z, t, m, n0, mid, wg, wo, n1, wp)


def finish(sh, zt, t, n0, mid, wg, wo):
    return pl.pallas_call(
        _finish_kernel, grid=sh.grid, out_shape=jax.ShapeDtypeStruct((sh.rows, sh.width, sh.cz), BF16),
        in_specs=[sh.zt_spec, sh.t_spec] + [_whole(a) for a in (n0, mid, wg, wo)],
        out_specs=sh.z_spec, scratch_shapes=[sh.scr_y], compiler_params=PARAMS,
        cost_estimate=_cost(sh.f_fin * 8, sh.bytes), name="finish",
    )(zt, t, n0, mid, wg, wo)


def triangle(sh, sides, contract):
    side = lambda s: pl.BlockSpec((sh.n, 1, 1, sh.rows, sh.width), lambda c: (0, s, c, 0, 0))
    return pl.pallas_call(
        functools.partial(_triangle_kernel, contract), grid=(sh.cl,), out_shape=sh.tri,
        in_specs=[side(0), side(1)], out_specs=pl.BlockSpec((sh.n, 1, sh.rows, sh.width), lambda c: (0, c, 0, 0)),
        compiler_params=PARAMS, cost_estimate=_cost(sh.f_tri * 8, sh.bytes), name="triangle",
    )(sides, sides)


def exchange(v):
    return lax.all_to_all(v, "dap", 0, 0, tiled=True)


def _lanes(norm):
    return jnp.broadcast_to(norm.astype(F32)[..., None], norm.shape + (LANES,))


def solution(mesh):
    n = mesh.shape["dap"]
    row_spec = P(("data", "dap"), None, None)
    mask_spec = P(("data", "dap"), None)
    rep = P()

    def per_device(z_one, mask_one, z_two, mask_two, norm_in, w_proj, w_gate, norm_mid, w_out):
        sh = Shapes(n, z_one, w_proj)
        nin, mid = _lanes(norm_in), _lanes(norm_mid)
        wp, wg, wo = (jnp.swapaxes(w, 1, 2) for w in (w_proj, w_gate, w_out))
        zs, ms = (z_one, z_two), (mask_one, mask_two)
        sides = [project(sh, z, m, nin[0], wp[0]) for z, m in zip(zs, ms)]
        got = [exchange(s) for s in sides]
        tri = [exchange(triangle(sh, g, 1)) for g in got]
        mids = [finish_project(sh, z, t, m, nin[0], mid[0], wg[0], wo[0], nin[1], wp[1]) for z, t, m in zip(zs, tri, ms)]
        got = [exchange(s) for _, s in mids]
        tri = [exchange(triangle(sh, g, 0)) for g in got]
        return tuple(finish(sh, zt, t, nin[1], mid[1], wg[1], wo[1]) for (zt, _), t in zip(mids, tri))

    return jax.shard_map(per_device, mesh=mesh,
                         in_specs=(row_spec, mask_spec, row_spec, mask_spec, rep, rep, rep, rep, rep),
                         out_specs=(row_spec, row_spec), check_vma=False)
```

time: 1030 us -> 937 us (0.910)
  Pallas kernels: 0 us -> 420 us
  local copies, waits for them, and re-layouts: 242 us -> 5.78 us
  matrix products: 131 us -> 0 us
  other arithmetic: 126 us -> 0.69 us
    pallas_call x0 -> x10, Pallas kernels: none -> 420 us  [the longest x2 177 us: finish_project(): pl.pallas_call(_finish_project_kernel, grid=sh.grid, out_shape=(sh.zt, sh...]
    convert_element_type x20 -> x0, local copies, waits for them, and re-layouts: 152 us -> none  [the longest x4 95.7 us: project_rows(): (keep_mask * jax.nn.sigmoid(projected[:, 1]) * projected[:, 0]).astype(jn...]
    dot_general x16 -> x0, matrix products: 131 us -> none  [the longest x4 61.9 us: project_rows(): jnp.einsum('rnz,zsgc->sgcrn', x_norm, w_split, preferred_element_type=jnp...]
    convert_element_type x9 -> x2, other arithmetic: 84.6 us -> 0.69 us  [_lanes(): return jnp.broadcast_to(norm.astype(F32)[..., None], norm.shape + (LANES,))]
    reduce_sum x14 -> x0, other arithmetic: 40.5 us -> none  [the longest x8 23.9 us: layer_norm(): row_var = jnp.mean(centred * centred, axis=feature_axis, keepdims=True)]
    all_to_all x6 -> x0, local copies, waits for them, and re-layouts: 40.2 us -> none  [the longest x4 34.3 us: tri_update(): sides_chan = lax.all_to_all(sides, 'dap', 1, 2, tiled=True)]
    unnamed x74 -> x9, local copies, waits for them, and re-layouts: 29.2 us -> 1.37 us
    slice x13 -> x0, local copies, waits for them, and re-layouts: 20.7 us -> none  [the longest x8 18.8 us: tri_update(): sides_chan[1]]
  transfers between devices with their start and end apart: 8 -> 8, of which waited for: 8 -> 7; matrix products, arithmetic and copies ran while one was open for 27% -> 0% of each run, Pallas kernels for 0% -> 34%
where the time goes in v1:
time: 937 us; the launch traced here: 932 us
  Pallas kernels  420 us (45%)
  waiting for transfers between devices  413 us (44%)
  starting transfers between devices  91.1 us (10%)
    all_to_all x8, waiting for transfers between devices, exchange(): return lax.all_to_all(v, 'dap', 0, 0, tiled=True)  413 us
    pallas_call x2, Pallas kernels, finish_project(): pl.pallas_call(_finish_project_kernel, grid=sh.grid, out_shape=(sh.zt, sh...  177 us
    pallas_call x2, Pallas kernels, project(): pl.pallas_call(_project_kernel, grid=sh.grid, out_shape=sh.sides, in_spec...  108 us
    pallas_call x2, Pallas kernels, finish(): pl.pallas_call(_finish_kernel, grid=sh.grid, out_shape=jax.ShapeDtypeStru...  102 us
    all_to_all x8, starting transfers between devices, exchange(): return lax.all_to_all(v, 'dap', 0, 0, tiled=True)  91.1 us
    pallas_call x4, Pallas kernels, triangle(): pl.pallas_call(functools.partial(_triangle_kernel, contract), grid=(sh.cl...  33.3 us
  transfers between devices with their start and end apart: 8, of which 7 were waited for; matrix products, arithmetic and copies ran while one was open for 0% of the time, Pallas kernels for 34%

profile of v1, /device:TPU:97, one launch (start us, length us, event | category | flops | bytes accessed | tf_op | source)
XLA Modules:
  0.0 931.8 jit_solution(13328081516814478251)
XLA Ops:
  0.6 0.7 convert_element_type.6
  1.3 1.1 copy.11
  2.4 0.7 slice_bitcast_fusion
  3.2 0.7 broadcast_in_dim.25.norm_ref.n0_ref
  3.9 53.9 %project.2 = bf16[32,2,4,24,768]{4,3,2,1,0:T(8,128)(2,1)} custom-call(bf16[24,768,128]{2,1,0:T(8,128)(2,1)} %z_ref.5, s32[24,768]{1,0:T(8,128)} %m_ref.5, f32[2,128,128]{2,1,0:T(8,128)} %broadcast_in_dim.25.norm_ref.n0_ref, bf16[512,128]{1,0:T(8,128)(2,1)} %get-tuple-element.11.wp_ref), custom_call_target="tpu_custom_call" | custom-call | flops 19327352832 | bytes 18874368 | tf_op jit(solution)/shard_map/project/pallas_call | solution.py:166
  57.8 9.1 all-to-all-start
  66.9 53.8 %project.3 = bf16[32,2,4,24,768]{4,3,2,1,0:T(8,128)(2,1)} custom-call(bf16[24,768,128]{2,1,0:T(8,128)(2,1)} %z_ref.7, s32[24,768]{1,0:T(8,128)} %m_ref.7, f32[2,128,128]{2,1,0:T(8,128)} %broadcast_in_dim.25.norm_ref.n0_ref, bf16[512,128]{1,0:T(8,128)(2,1)} %get-tuple-element.11.wp_ref), custom_call_target="tpu_custom_call" | custom-call | flops 19327352832 | bytes 18874368 | tf_op jit(solution)/shard_map/project/pallas_call | solution.py:166
  120.7 63.6 %all-to-all-done.a_ref.b_ref = bf16[32,2,4,24,768]{4,3,2,1,0:T(8,128)(2,1)} async-done(((bf16[32,2,4,24,768]{4,3,2,1,0:T(8,128)(2,1)}), bf16[32,2,4,24,768]{4,3,2,1,0:T(8,128)(2,1)}, u32[]{:S(2)}, u32[]{:S(2)}) %all-to-all-start) | async-done | bytes 9437216 | tf_op jit(solution)/shard_map/all_to_all | solution.py:201
  184.3 14.1 %all-to-all-start.4 = ((bf16[32,2,4,24,768]{4,3,2,1,0:T(8,128)(2,1)}), bf16[32,2,4,24,768]{4,3,2,1,0:T(8,128)(2,1)}, u32[]{:S(2)}, u32[]{:S(2)}) async-start(bf16[32,2,4,24,768]{4,3,2,1,0:T(8,128)(2,1)} %project.3), calls=%async_computation.4 | async-start | bytes 18874368 | tf_op jit(solution)/shard_map/all_to_all | solution.py:201
  198.4 8.3 triangle.4
  206.7 107.7 %all-to-all-done.4.a_ref.b_ref = bf16[32,2,4,24,768]{4,3,2,1,0:T(8,128)(2,1)} async-done(((bf16[32,2,4,24,768]{4,3,2,1,0:T(8,128)(2,1)}), bf16[32,2,4,24,768]{4,3,2,1,0:T(8,128)(2,1)}, u32[]{:S(2)}, u32[]{:S(2)}) %all-to-all-start.4) | async-done | bytes 9437216 | tf_op jit(solution)/shard_map/all_to_all | solution.py:201
  314.5 15.5 %all-to-all-start.1 = ((bf16[32,4,24,768]{3,2,1,0:T(8,128)(2,1)}), bf16[32,4,24,768]{3,2,1,0:T(8,128)(2,1)}, u32[]{:S(2)}, u32[]{:S(2)}) async-start(bf16[32,4,24,768]{3,2,1,0:T(8,128)(2,1)} %triangle.4), calls=%async_computation.1 | async-start | bytes 9437184 | tf_op jit(solution)/shard_map/all_to_all | solution.py:201
  329.9 8.3 triangle.6
  338.2 0.0 copy-start.2
  338.2 0.0 copy-start
  338.2 0.0 copy-start.1
  338.2 49.5 %all-to-all-done.1.t_ref = bf16[32,4,24,768]{3,2,1,0:T(8,128)(2,1)} async-done(((bf16[32,4,24,768]{3,2,1,0:T(8,128)(2,1)}), bf16[32,4,24,768]{3,2,1,0:T(8,128)(2,1)}, u32[]{:S(2)}, u32[]{:S(2)}) %all-to-all-start.1) | async-done | bytes 4718624 | tf_op jit(solution)/shard_map/all_to_all | solution.py:201
  387.7 8.5 all-to-all-start.5
  396.2 0.0 copy-done.2
  396.2 0.0 copy-done
  396.2 0.1 copy.13
  396.4 0.0 copy-done.1
  396.4 0.1 copy.12
  396.5 0.7 slice_bitcast_fusion.2
  397.2 0.8 broadcast_in_dim.27.mid_ref
  397.9 0.7 broadcast_in_dim.29.n1_ref.n0_ref
  398.7 88.7 %finish_project.2 = (bf16[24,128,768]{2,1,0:T(8,128)(2,1)}, bf16[32,2,4,24,768]{4,3,2,1,0:T(8,128)(2,1)}) custom-call(bf16[24,768,128]{2,1,0:T(8,128)(2,1)} %z_ref.5, bf16[32,4,24,768]{3,2,1,0:T(8,128)(2,1)} %all-to-all-done.1.t_ref, s32[24,768]{1,0:T(8,128)} %m_ref.5, f32[2,128,128]{2,1,0:T(8,128)} %broadcast_in_dim.25.norm_ref.n0_ref, ...), custom_call_target="tpu_custom_call" | custom-call | flops 28991029248 | bytes 37748736 | tf_op jit(solution)/shard_map/finish_project/pallas_call | solution.py:174
  487.4 0.0 all-to-all-done.5.t_ref
  487.4 6.4 all-to-all-start.2
  493.7 88.6 %finish_project.3 = (bf16[24,128,768]{2,1,0:T(8,128)(2,1)}, bf16[32,2,4,24,768]{4,3,2,1,0:T(8,128)(2,1)}) custom-call(bf16[24,768,128]{2,1,0:T(8,128)(2,1)} %z_ref.7, bf16[32,4,24,768]{3,2,1,0:T(8,128)(2,1)} %all-to-all-done.5.t_ref, s32[24,768]{1,0:T(8,128)} %m_ref.7, f32[2,128,128]{2,1,0:T(8,128)} %broadcast_in_dim.25.norm_ref.n0_ref, ...), custom_call_target="tpu_custom_call" | custom-call | flops 28991029248 | bytes 37748736 | tf_op jit(solution)/shard_map/finish_project/pallas_call | solution.py:174
  582.4 28.8 %all-to-all-done.2.a_ref.b_ref = bf16[32,2,4,24,768]{4,3,2,1,0:T(8,128)(2,1)} async-done(((bf16[32,2,4,24,768]{4,3,2,1,0:T(8,128)(2,1)}), bf16[32,2,4,24,768]{4,3,2,1,0:T(8,128)(2,1)}, u32[]{:S(2)}, u32[]{:S(2)}) %all-to-all-start.2) | async-done | bytes 9437216 | tf_op jit(solution)/shard_map/all_to_all | solution.py:201
  611.2 14.1 %all-to-all-start.6 = ((bf16[32,2,4,24,768]{4,3,2,1,0:T(8,128)(2,1)}), bf16[32,2,4,24,768]{4,3,2,1,0:T(8,128)(2,1)}, u32[]{:S(2)}, u32[]{:S(2)}) async-start(bf16[32,2,4,24,768]{4,3,2,1,0:T(8,128)(2,1)} %get-tuple-element.9), calls=%async_computation.6 | async-start | bytes 18874368 | tf_op jit(solution)/shard_map/all_to_all | solution.py:201
  625.3 8.3 triangle.5
  633.6 107.7 %all-to-all-done.6.a_ref.b_ref = bf16[32,2,4,24,768]{4,3,2,1,0:T(8,128)(2,1)} async-done(((bf16[32,2,4,24,768]{4,3,2,1,0:T(8,128)(2,1)}), bf16[32,2,4,24,768]{4,3,2,1,0:T(8,128)(2,1)}, u32[]{:S(2)}, u32[]{:S(2)}) %all-to-all-start.6) | async-done | bytes 9437216 | tf_op jit(solution)/shard_map/all_to_all | solution.py:201
  741.3 15.5 %all-to-all-start.3 = ((bf16[32,4,24,768]{3,2,1,0:T(8,128)(2,1)}), bf16[32,4,24,768]{3,2,1,0:T(8,128)(2,1)}, u32[]{:S(2)}, u32[]{:S(2)}) async-start(bf16[32,4,24,768]{3,2,1,0:T(8,128)(2,1)} %triangle.5), calls=%async_computation.3 | async-start | bytes 9437184 | tf_op jit(solution)/shard_map/all_to_all | solution.py:201
  756.8 8.4 triangle.7
  765.2 49.9 %all-to-all-done.3.t_ref = bf16[32,4,24,768]{3,2,1,0:T(8,128)(2,1)} async-done(((bf16[32,4,24,768]{3,2,1,0:T(8,128)(2,1)}), bf16[32,4,24,768]{3,2,1,0:T(8,128)(2,1)}, u32[]{:S(2)}, u32[]{:S(2)}) %all-to-all-start.3) | async-done | bytes 4718624 | tf_op jit(solution)/shard_map/all_to_all | solution.py:201
  815.0 8.0 all-to-all-start.7
  823.0 0.8 broadcast_in_dim.31.mid_ref
  823.8 50.9 %finish.2 = bf16[24,768,128]{2,1,0:T(8,128)(2,1)} custom-call(bf16[24,128,768]{2,1,0:T(8,128)(2,1)} %get-tuple-element.6.zt_ref, bf16[32,4,24,768]{3,2,1,0:T(8,128)(2,1)} %all-to-all-done.3.t_ref, f32[2,128,128]{2,1,0:T(8,128)} %broadcast_in_dim.29.n1_ref.n0_ref, f32[2,128,128]{2,1,0:T(8,128)} %broadcast_in_dim.31.mid_ref, ...), custom_call_target="tpu_custom_call" | custom-call | flops 9663676416 | bytes 18874368 | tf_op jit(solution)/shard_map/finish/pallas_call | solution.py:183
  874.7 6.0 all-to-all-done.7.t_ref
  880.8 51.1 %finish.3 = bf16[24,768,128]{2,1,0:T(8,128)(2,1)} custom-call(bf16[24,128,768]{2,1,0:T(8,128)(2,1)} %get-tuple-element.8.zt_ref, bf16[32,4,24,768]{3,2,1,0:T(8,128)(2,1)} %all-to-all-done.7.t_ref, f32[2,128,128]{2,1,0:T(8,128)} %broadcast_in_dim.29.n1_ref.n0_ref, f32[2,128,128]{2,1,0:T(8,128)} %broadcast_in_dim.31.mid_ref, ...), custom_call_target="tpu_custom_call" | custom-call | flops 9663676416 | bytes 18874368 | tf_op jit(solution)/shard_map/finish/pallas_call | solution.py:183
  (3 shorter events, 0.0 us)
Async XLA Ops:
  57.8 126.6 %all-to-all-start = ((bf16[32,2,4,24,768]{4,3,2,1,0:T(8,128)(2,1)}), bf16[32,2,4,24,768]{4,3,2,1,0:T(8,128)(2,1)}, u32[]{:S(2)}, u32[]{:S(2)}) async-start(bf16[32,2,4,24,768]{4,3,2,1,0:T(8,128)(2,1)} %project.2), calls=%async_computation | async-start | bytes 18874368 | tf_op jit(solution)/shard_map/all_to_all | solution.py:201
  184.3 130.1 %all-to-all-start.4 = ((bf16[32,2,4,24,768]{4,3,2,1,0:T(8,128)(2,1)}), bf16[32,2,4,24,768]{4,3,2,1,0:T(8,128)(2,1)}, u32[]{:S(2)}, u32[]{:S(2)}) async-start(bf16[32,2,4,24,768]{4,3,2,1,0:T(8,128)(2,1)} %project.3), calls=%async_computation.4 | async-start | bytes 18874368 | tf_op jit(solution)/shard_map/all_to_all | solution.py:201
  314.5 73.3 %all-to-all-start.1 = ((bf16[32,4,24,768]{3,2,1,0:T(8,128)(2,1)}), bf16[32,4,24,768]{3,2,1,0:T(8,128)(2,1)}, u32[]{:S(2)}, u32[]{:S(2)}) async-start(bf16[32,4,24,768]{3,2,1,0:T(8,128)(2,1)} %triangle.4), calls=%async_computation.1 | async-start | bytes 9437184 | tf_op jit(solution)/shard_map/all_to_all | solution.py:201
  338.2 58.0 %copy-start.2 = (bf16[2,2,128]{2,1,0:T(2,128)(2,1)S(1)}, bf16[2,2,128]{2,1,0:T(2,128)(2,1)}, u32[]{:S(2)}) copy-start(bf16[2,2,128]{2,1,0:T(2,128)(2,1)} %param.16) | copy-start | bytes 3076
  338.2 58.0 %copy-start = (bf16[2,128,128]{2,1,0:T(8,128)(2,1)S(1)}, bf16[2,128,128]{2,1,0:T(8,128)(2,1)}, u32[]{:S(2)}) copy-start(bf16[2,128,128]{2,1,0:T(8,128)(2,1)} %param.17) | copy-start | bytes 196612
  338.2 58.1 %copy-start.1 = (bf16[2,128,128]{2,1,0:T(8,128)(2,1)S(1)}, bf16[2,128,128]{2,1,0:T(8,128)(2,1)}, u32[]{:S(2)}) copy-start(bf16[2,128,128]{2,1,0:T(8,128)(2,1)} %param.15) | copy-start | bytes 196612
  387.7 99.7 %all-to-all-start.5 = ((bf16[32,4,24,768]{3,2,1,0:T(8,128)(2,1)}), bf16[32,4,24,768]{3,2,1,0:T(8,128)(2,1)}, u32[]{:S(2)}, u32[]{:S(2)}) async-start(bf16[32,4,24,768]{3,2,1,0:T(8,128)(2,1)} %triangle.6), calls=%async_computation.5 | async-start | bytes 9437184 | tf_op jit(solution)/shard_map/all_to_all | solution.py:201
  487.4 123.8 %all-to-all-start.2 = ((bf16[32,2,4,24,768]{4,3,2,1,0:T(8,128)(2,1)}), bf16[32,2,4,24,768]{4,3,2,1,0:T(8,128)(2,1)}, u32[]{:S(2)}, u32[]{:S(2)}) async-start(bf16[32,2,4,24,768]{4,3,2,1,0:T(8,128)(2,1)} %get-tuple-element.7), calls=%async_computation.2 | async-start | bytes 18874368 | tf_op jit(solution)/shard_map/all_to_all | solution.py:201
  611.2 130.1 %all-to-all-start.6 = ((bf16[32,2,4,24,768]{4,3,2,1,0:T(8,128)(2,1)}), bf16[32,2,4,24,768]{4,3,2,1,0:T(8,128)(2,1)}, u32[]{:S(2)}, u32[]{:S(2)}) async-start(bf16[32,2,4,24,768]{4,3,2,1,0:T(8,128)(2,1)} %get-tuple-element.9), calls=%async_computation.6 | async-start | bytes 18874368 | tf_op jit(solution)/shard_map/all_to_all | solution.py:201
  741.3 73.7 %all-to-all-start.3 = ((bf16[32,4,24,768]{3,2,1,0:T(8,128)(2,1)}), bf16[32,4,24,768]{3,2,1,0:T(8,128)(2,1)}, u32[]{:S(2)}, u32[]{:S(2)}) async-start(bf16[32,4,24,768]{3,2,1,0:T(8,128)(2,1)} %triangle.5), calls=%async_computation.3 | async-start | bytes 9437184 | tf_op jit(solution)/shard_map/all_to_all | solution.py:201
  815.0 65.7 %all-to-all-start.7 = ((bf16[32,4,24,768]{3,2,1,0:T(8,128)(2,1)}), bf16[32,4,24,768]{3,2,1,0:T(8,128)(2,1)}, u32[]{:S(2)}, u32[]{:S(2)}) async-start(bf16[32,4,24,768]{3,2,1,0:T(8,128)(2,1)} %triangle.7), calls=%async_computation.7 | async-start | bytes 9437184 | tf_op jit(solution)/shard_map/all_to_all | solution.py:201

commit v2 on v0

v2 whole, which is shorter than its diff:
```python
import functools
import math

import jax
import jax.numpy as jnp
from jax import lax
from jax.experimental import pallas as pl
from jax.experimental.pallas import tpu as pltpu
from jax.sharding import PartitionSpec as P

RB = 8
LANES = 128
UNROLL = 4
F32, BF16 = jnp.float32, jnp.bfloat16


def _norm_cols(v, gain, shift):
    mean = jnp.mean(v, axis=0, keepdims=True)
    cen = v - mean
    var = jnp.mean(cen * cen, axis=0, keepdims=True)
    return (cen * lax.rsqrt(var + 1e-5) * gain + shift).astype(BF16)


def _mm(a, b):
    return lax.dot_general(a, b, (((1,), (0,)), ((), ())), preferred_element_type=F32)


def _project(z_t, norm_ref, wp_ref, scr, r, kk):
    hid = wp_ref.shape[0] // 4
    x_t = _norm_cols(z_t, norm_ref[0], norm_ref[1])
    q = _mm(wp_ref[...], x_t)
    for s in range(2):
        p, g = q[2 * s * hid:(2 * s + 1) * hid], q[(2 * s + 1) * hid:(2 * s + 2) * hid]
        scr[kk, pl.ds(s * hid * RB + r, hid, stride=RB), :] = jax.nn.sigmoid(g) * p


def _emit_sides(scr, m_ref, out_ref, kk, topo):
    half = scr.shape[1] // 2
    lanes = slice(kk * LANES, (kk + 1) * LANES)
    keep = m_ref[:, lanes].astype(F32)
    for q in range(topo.nq):
        for rho, owner in topo.blocks(q):
            for s in range(2):
                at = pl.multiple_of(s * half + (owner * topo.nq + q) * RB, RB)
                out_ref[(q, s) + rho + (slice(None), lanes)] = (scr[kk, pl.ds(at, RB), :] * keep).astype(BF16)


def _finish(z_t, r, kk, scr_y, norm_ref, mid_ref, wg_ref, wo_ref):
    hid = wo_ref.shape[1]
    x_t = _norm_cols(z_t, norm_ref[0], norm_ref[1])
    gate = jax.nn.sigmoid(_mm(wg_ref[...], x_t))
    y = scr_y[kk, pl.ds(r, hid, stride=RB), :]
    y = (y * mid_ref[0] + mid_ref[1]).astype(BF16)
    return (z_t + gate * _mm(wo_ref[...], y)).astype(BF16)


def _norm_mid(t_refs, scr_y, kk, topo):
    lanes = slice(kk * LANES, (kk + 1) * LANES)
    tiles = [(q,) + rest for q in range(topo.nq) for rest in topo.landed(q)]
    inv_n = 1.0 / len(tiles)

    def load(tile):
        return t_refs[tile[1]][(tile[0],) + tile[2] + (slice(None), lanes)].astype(F32)

    def total(f):
        part = [f(load(t)) for t in tiles[:4]]
        for i, t in enumerate(tiles[4:]):
            part[i % 4] = part[i % 4] + f(load(t))
        return (part[0] + part[1]) + (part[2] + part[3])
    mean = total(lambda v: v) * inv_n
    inv = lax.rsqrt(total(lambda v: (v - mean) * (v - mean)) * inv_n + 1e-5)
    for t in tiles:
        at = pl.multiple_of((t[3] * topo.nq + t[0]) * RB, RB)
        scr_y[kk, pl.ds(at, RB), :] = (load(t) - mean) * inv


def _row_loop(width, f):
    def body(i, c):
        for u in range(UNROLL):
            for kk in range(width // LANES):
                f(i * UNROLL + u, kk, slice(kk * LANES, (kk + 1) * LANES))
        return c
    lax.fori_loop(0, RB // UNROLL, body, 0)


class Topo:
    def __init__(self, n):
        self.side = math.isqrt(n // 2)
        ring = self.side.bit_length() - 1
        self.nq = 2 * ring
        self.nb = self.nq + 1
        links = [(axis, bit) for bit in range(ring) for axis in ("x", "y")]
        self.order = [[("core", 0)] + [links[(q + i) % self.nq] for i in range(self.nq)] for q in range(self.nq)]
        self.weight = {("core", 0): 1}
        self.weight.update({("x", b): 2 << b for b in range(ring)})
        self.weight.update({("y", b): (2 << ring) << b for b in range(ring)})

    def here(self):
        me = lax.axis_index("dap")
        self.pos = {"core": lax.rem(me, 2), "x": lax.rem(me // 2, self.side), "y": me // (2 * self.side)}
        self.bit = {}
        for axis, b in self.weight:
            v = self.pos[axis]
            self.bit[axis, b] = lax.rem(v // (1 << b) + v // (2 << b), 2) if axis != "core" else v
        return self

    def partner(self, link):
        axis, b = link
        pos = dict(self.pos)
        v, span = pos[axis], 2 << b
        base = v - lax.rem(v, span)
        pos[axis] = base + (span - 1) - lax.rem(v, span)
        return (pos["y"] * self.side + pos["x"]) * 2 + pos["core"]

    def blocks(self, q):
        out = [((), 0)]
        for link in self.order[q]:
            w, own = self.weight[link], self.bit[link]
            out = [(r + (f,), o + w * (1 - own if f else own)) for r, o in out for f in (0, 1)]
        return out

    def landed(self, q):
        out = []
        for rho, owner in self.blocks(q):
            last = max([i for i, f in enumerate(rho) if f], default=-1)
            idx = (0,) * self.nb if last < 0 else rho[:last] + (0,) * (self.nb - last)
            out.append((last + 1, idx, owner))
        return out

    def natural(self, owner):
        side, core, rest = self.side, lax.rem(owner, 2), owner // 2
        gx, gy = lax.rem(rest, side), rest // side

        def binary(g):
            v, b = 0, 0
            k = side.bit_length() - 2
            for i in range(k, -1, -1):
                b = lax.rem(b + lax.rem(g // (1 << i), 2), 2)
                v = v + b * (1 << i)
            return v
        return (binary(gy) * side + binary(gx)) * 2 + core

    def gray_bits(self, p):
        pos = {"core": p % 2, "x": p // 2 % self.side, "y": p // 2 // self.side}
        return {k: (pos[k[0]] if k[0] == "core" else (pos[k[0]] >> k[1] ^ pos[k[0]] >> (k[1] + 1)) & 1) for k in self.weight}

    def relative(self, q, p):
        bits = self.gray_bits(p)
        return tuple((1 - self.bit[k]) if bits[k] else self.bit[k] for k in self.order[q])


class Exchange:
    def __init__(self, topo, src, dst, ssem, rsem):
        self.topo, self.src, self.dst, self.ssem, self.rsem = topo, src, dst, ssem, rsem
        self.cut = src.shape[1] == 1

    def _tail(self, sub):
        if not self.cut:
            return sub, ()
        w = self.src.shape[-1] // 2
        return 0, (slice(None), pl.ds(sub * w, w))

    def _copy(self, q, sub, s, a, b):
        return pltpu.make_async_remote_copy(
            src_ref=a, dst_ref=b, send_sem=self.ssem.at[q, sub, s], recv_sem=self.rsem.at[q, sub, s],
            device_id={"dap": self.topo.partner(self.topo.order[q][s])}, device_id_type=pl.DeviceIdType.MESH)

    def start(self, sub, s):
        nb, free = self.topo.nb, (slice(None),)
        k, tail = self._tail(sub)
        for q in range(self.topo.nq):
            for t in range(-1, s):
                if t < 0:
                    idx = (0,) * s + (1,) + free * (nb - 1 - s) + tail
                    a = self.src.at[(q, k) + idx]
                else:
                    idx = free * t + (1,) + (0,) * (s - 1 - t) + (1,) + free * (nb - 1 - s) + tail
                    a = self.dst.at[(q, k, t) + idx]
                self._copy(q, sub, s, a, self.dst.at[(q, k, s) + idx]).start()

    def _whole(self, q, sub, s):
        k, tail = self._tail(sub)
        ref = self.dst.at[(q, k, s) + (slice(None),) * s + (1,) + (slice(None),) * (self.topo.nb - 1 - s) + tail]
        return self._copy(q, sub, s, ref, ref)

    def arrive(self, sub, s):
        for q in range(self.topo.nq):
            self._whole(q, sub, s).wait_recv()

    def drain(self):
        for sub in range(2):
            for s in range(self.topo.nb):
                for q in range(self.topo.nq):
                    self._whole(q, sub, s).wait_send()

    def barrier(self):
        bar = pltpu.get_barrier_semaphore()
        for link in self.topo.weight:
            pl.semaphore_signal(bar, inc=1, device_id={"dap": self.topo.partner(link)}, device_id_type=pl.DeviceIdType.MESH)
        pl.semaphore_wait(bar, len(self.topo.weight))

    def moves(self):
        out = []
        for s in range(self.topo.nb):
            for sub in range(2):
                def move(s=s, sub=sub):
                    self.arrive(sub, s)
                    if s + 1 < self.topo.nb:
                        self.start(sub, s + 1)
                out.append(move)
        return out


def _project_kernel(topo, z_ref, m_ref, norm_ref, wp_ref, out_ref, scr):
    def row(r, kk, lanes):
        _project(z_ref[r, lanes, :].astype(F32).T, norm_ref, wp_ref, scr, r, kk)
    _row_loop(z_ref.shape[1], row)
    for kk in range(z_ref.shape[1] // LANES):
        _emit_sides(scr, m_ref, out_ref, kk, topo)


def _finish_project_kernel(topo, z_ref, m_ref, n0_ref, mid_ref, wg_ref, wo_ref, n1_ref, wp_ref, *refs):
    t_refs, (zt_ref, out_ref, scr_y, scr) = refs[:-4], refs[-4:]
    for kk in range(z_ref.shape[1] // LANES):
        _norm_mid(t_refs, scr_y, kk, topo)

    def row(r, kk, lanes):
        z_t = z_ref[r, lanes, :].astype(F32).T
        z_new = _finish(z_t, r, kk, scr_y, n0_ref, mid_ref, wg_ref, wo_ref)
        zt_ref[r, :, lanes] = z_new
        _project(z_new.astype(F32), n1_ref, wp_ref, scr, r, kk)
    _row_loop(z_ref.shape[1], row)
    for kk in range(z_ref.shape[1] // LANES):
        _emit_sides(scr, m_ref, out_ref, kk, topo)


def _finish_kernel(topo, zt_ref, n0_ref, mid_ref, wg_ref, wo_ref, *refs):
    t_refs, (z_ref, scr_y) = refs[:-2], refs[-2:]
    for kk in range(z_ref.shape[1] // LANES):
        _norm_mid(t_refs, scr_y, kk, topo)

    def row(r, kk, lanes):
        z_new = _finish(zt_ref[r, :, lanes].astype(F32), r, kk, scr_y, n0_ref, mid_ref, wg_ref, wo_ref)
        z_ref[r, lanes, :] = z_new.astype(F32).T.astype(BF16)
    _row_loop(z_ref.shape[1], row)


def _triangle_kernel(topo, contract, *refs):
    half = (len(refs) - 3) // 2
    a_refs, b_refs, (out_ref, a_scr, b_scr) = refs[:half], refs[half:2 * half], refs[-3:]
    n, rows, width = a_scr.shape
    step = pl.program_id(0)

    def gather(q):
        for i, (piece, idx, owner) in enumerate(topo.landed(q)):
            a_scr[i] = a_refs[piece][(0,) + idx]
            b_scr[topo.natural(owner) if contract else i] = b_refs[piece][(0,) + idx]

    def scatter(q):
        for p in range(n):
            out_ref[(0,) + topo.relative(q, p)] = a_scr[p]
    for q in range(topo.nq):
        pl.when(step == q)(functools.partial(gather, q))
    a, b = a_scr[...].reshape(n * rows, width), b_scr[...].reshape(n * rows, width)
    t = lax.dot_general(a, b, (((contract,), (contract,)), ((), ())), preferred_element_type=F32)
    t = t.astype(BF16).reshape(n, rows, width)
    if contract:
        out_ref[...] = t.reshape(out_ref.shape)
    else:
        a_scr[...] = t
        for q in range(topo.nq):
            pl.when(step == q)(functools.partial(scatter, q))


def _whole(a):
    return pl.BlockSpec(a.shape, lambda *_: (0,) * a.ndim)


class Shapes:
    def __init__(self, n, z, w_proj):
        self.topo = topo = Topo(n)
        self.n, (self.rows, self.width, self.cz) = n, z.shape
        self.hid = w_proj.shape[-1] // 4
        assert self.hid == n * topo.nq
        self.kb = 2 * LANES if self.width % (2 * LANES) == 0 else LANES
        self.grid = (self.rows // RB, self.width // self.kb)
        self.bits = (2,) * topo.nb
        zero = (0,) * topo.nb
        self.z_spec = pl.BlockSpec((RB, self.kb, self.cz), lambda i, j: (i, j, 0))
        self.zt_spec = pl.BlockSpec((RB, self.cz, self.kb), lambda i, j: (i, 0, j))
        self.m_spec = pl.BlockSpec((RB, self.kb), lambda i, j: (i, j))
        self.sides_spec = pl.BlockSpec((topo.nq, 2) + self.bits + (RB, self.kb), lambda i, j: (0, 0) + zero + (i, j))
        self.sides = jax.ShapeDtypeStruct((topo.nq, 2) + self.bits + (self.rows, self.width), BF16)
        self.tri = jax.ShapeDtypeStruct((topo.nq, 1) + self.bits + (self.rows, self.width), BF16)
        self.zt = jax.ShapeDtypeStruct((self.rows, self.cz, self.width), BF16)
        self.scr = pltpu.VMEM((self.kb // LANES, 2 * self.hid * RB, LANES), F32)
        self.scr_y = pltpu.VMEM((self.kb // LANES, self.hid * RB, LANES), F32)
        self.mat = pltpu.VMEM((n, self.rows, self.width), BF16)

    def landing(self, src):
        return jax.ShapeDtypeStruct(src.shape[:2] + (self.topo.nb,) + src.shape[2:], BF16)

    def _pieces(self, head, tail, index):
        nb = self.topo.nb
        specs = [pl.BlockSpec((head, None) + (1,) * nb + tail, lambda *g: index(g)[0] + (0,) * nb + index(g)[1])]
        for s in range(nb):
            at = (0,) * s + (1,) + (0,) * (nb - 1 - s)
            specs.append(pl.BlockSpec((head, None, None) + (2,) * s + (1,) * (nb - s) + tail,
                                      lambda *g, s=s, at=at: index(g)[0] + (s,) + at + index(g)[1]))
        return specs

    def tri_pieces(self):
        return self._pieces(self.topo.nq, (RB, self.kb), lambda g: ((0, 0), (g[0], g[1])))

    def side_pieces(self, side):
        return self._pieces(1, (self.rows, self.width), lambda g: ((g[0], side), (0, 0)))


def call(sh, name, body, grid, ins, in_specs, outs, out_specs, scratch, moving=None, cid=0, pace=None):
    topo = sh.topo
    steps = math.prod(grid)
    params = dict(vmem_limit_bytes=62 * 1024 * 1024)
    hbm = pl.BlockSpec(memory_space=pl.ANY)
    n_in, n_out = len(ins), len(outs)
    if moving is not None:
        ins, in_specs = list(ins) + [moving], list(in_specs) + [hbm]
        outs, out_specs = list(outs) + [sh.landing(moving)], list(out_specs) + [hbm]
        sems = pltpu.SemaphoreType.DMA((topo.nq, 2, topo.nb))
        scratch = list(scratch) + [sems, sems]
        params.update(collective_id=cid, has_side_effects=True)

    def kernel(*refs):
        topo.here()
        if moving is None:
            body(topo, *refs)
            return
        work = refs[:n_in] + refs[n_in + 1:n_in + 1 + n_out] + refs[n_in + n_out + 2:-2]
        ex = Exchange(topo, refs[n_in], refs[n_in + 1 + n_out], refs[-2], refs[-1])
        step = pl.program_id(0)
        for d, size in enumerate(grid[1:], 1):
            step = step * size + pl.program_id(d)

        @pl.when(step == 0)
        def _():
            ex.barrier()
            for sub in range(2):
                ex.start(sub, 0)
        moves = ex.moves()
        due = [max(1, int((i + 1) * pace)) if pace else steps for i in range(len(moves))]
        for g in range(1, steps):
            now = [m for m, d in zip(moves, due) if d == g]
            if now:
                pl.when(step == g)(lambda now=now: [m() for m in now] and None)
        body(topo, *work)

        @pl.when(step == steps - 1)
        def _():
            for m, d in zip(moves, due):
                if d >= steps:
                    m()
            ex.drain()

    return pl.pallas_call(kernel, grid=grid, out_shape=tuple(outs), in_specs=in_specs, out_specs=tuple(out_specs),
                          scratch_shapes=scratch, compiler_params=pltpu.CompilerParams(**params), name=name)(*ins)


def project(sh, z, m, norm, wp, **move):
    return call(sh, "project", _project_kernel, sh.grid, (z, m, norm, wp), [sh.z_spec, sh.m_spec, _whole(norm), _whole(wp)],
                [sh.sides], [sh.sides_spec], [sh.scr], **move)


def finish_project(sh, z, m, n0, mid, wg, wo, n1, wp, t, **move):
    flat = (n0, mid, wg, wo, n1, wp)
    return call(sh, "finish_project", _finish_project_kernel, sh.grid, (z, m) + flat + (t[0],) + (t[1],) * sh.topo.nb,
                [sh.z_spec, sh.m_spec] + [_whole(a) for a in flat] + sh.tri_pieces(),
                [sh.zt, sh.sides], [sh.zt_spec, sh.sides_spec], [sh.scr_y, sh.scr], **move)


def finish(sh, zt, n0, mid, wg, wo, t, **move):
    flat = (n0, mid, wg, wo)
    return call(sh, "finish", _finish_kernel, sh.grid, (zt,) + flat + (t[0],) + (t[1],) * sh.topo.nb,
                [sh.zt_spec] + [_whole(a) for a in flat] + sh.tri_pieces(),
                [jax.ShapeDtypeStruct((sh.rows, sh.width, sh.cz), BF16)], [sh.z_spec], [sh.scr_y], **move)


def triangle(sh, sides, contract, **move):
    nb = sh.topo.nb
    return call(sh, "triangle", lambda topo, *refs: _triangle_kernel(topo, contract, *refs), (sh.topo.nq,),
                ((sides[0],) + (sides[1],) * nb) * 2, sh.side_pieces(0) + sh.side_pieces(1),
                [sh.tri], [pl.BlockSpec((1, None) + sh.bits + (sh.rows, sh.width), lambda q: (q,) + (0,) * (nb + 3))],
                [sh.mat, sh.mat], **move)


def _lanes(norm):
    return jnp.broadcast_to(norm.astype(F32)[..., None], norm.shape + (LANES,))


def solution(mesh):
    n = mesh.shape["dap"]
    row_spec = P(("data", "dap"), None, None)
    mask_spec = P(("data", "dap"), None)
    rep = P()

    def per_device(z_one, mask_one, z_two, mask_two, norm_in, w_proj, w_gate, norm_mid, w_out):
        sh = Shapes(n, z_one, w_proj)
        nin, mid = _lanes(norm_in), _lanes(norm_mid)
        wp, wg, wo = (jnp.swapaxes(w, 1, 2) for w in (w_proj, w_gate, w_out))
        zs, ms = (z_one, z_two), (mask_one, mask_two)
        mask_a, mask_b = ms
        s1, = project(sh, zs[0], mask_a, nin[0], wp[0])
        s2, w1 = project(sh, zs[1], mask_b, nin[0], wp[0], moving=s1, cid=0)
        t1, w2 = triangle(sh, (s1, w1), 1, moving=s2, cid=1)
        t2, v1 = triangle(sh, (s2, w2), 1, moving=t1, cid=2)
        flat = (nin[0], mid[0], wg[0], wo[0], nin[1], wp[1])
        zt1, s1, v2 = finish_project(sh, zs[0], mask_a, *flat, (t1, v1), moving=t2, cid=3, pace=0.85)
        zt2, s2, w1 = finish_project(sh, zs[1], mask_b, *flat, (t2, v2), moving=s1, cid=4, pace=1.9)
        t1, w2 = triangle(sh, (s1, w1), 0, moving=s2, cid=5)
        t2, v1 = triangle(sh, (s2, w2), 0, moving=t1, cid=6)
        flat = (nin[1], mid[1], wg[1], wo[1])
        z1, v2 = finish(sh, zt1, *flat, (t1, v1), moving=t2, cid=7, pace=1.9)
        z2, = finish(sh, zt2, *flat, (t2, v2))
        return z1, z2

    return jax.shard_map(per_device, mesh=mesh,
                         in_specs=(row_spec, mask_spec, row_spec, mask_spec, rep, rep, rep, rep, rep),
                         out_specs=(row_spec, row_spec), check_vma=False)
```

time: 1030 us -> 787 us (0.76)
  Pallas kernels: 0 us -> 765 us
  waiting for transfers between devices: 417 us -> 0 us
  local copies, waits for them, and re-layouts: 242 us -> 11.9 us
  matrix products: 131 us -> 0 us
  other arithmetic: 126 us -> 0.68 us
  starting transfers between devices: 101 us -> 0 us
    pallas_call x0 -> x10, Pallas kernels: none -> 765 us  [call(): pl.pallas_call(kernel, grid=grid, out_shape=tuple(outs), in_specs=in_spec...]
    all_to_all x8 -> x0, waiting for transfers between devices: 417 us -> none  [the longest x4 259 us: tri_update(): sides_chan = lax.all_to_all(sides, 'dap', 1, 2, tiled=True)]
    convert_element_type x20 -> x0, local copies, waits for them, and re-layouts: 152 us -> none  [the longest x4 95.7 us: project_rows(): (keep_mask * jax.nn.sigmoid(projected[:, 1]) * projected[:, 0]).astype(jn...]
    dot_general x16 -> x0, matrix products: 131 us -> none  [the longest x4 61.9 us: project_rows(): jnp.einsum('rnz,zsgc->sgcrn', x_norm, w_split, preferred_element_type=jnp...]
    all_to_all x8 -> x0, starting transfers between devices: 101 us -> none  [the longest x4 50.6 us: tri_update(): t_rows = lax.all_to_all(tri_prod, 'dap', 1, 0, tiled=True)]
    convert_element_type x9 -> x2, other arithmetic: 84.6 us -> 0.68 us  [_lanes(): return jnp.broadcast_to(norm.astype(F32)[..., None], norm.shape + (LANES,))]
    reduce_sum x14 -> x0, other arithmetic: 40.5 us -> none  [the longest x8 23.9 us: layer_norm(): row_var = jnp.mean(centred * centred, axis=feature_axis, keepdims=True)]
    all_to_all x6 -> x0, local copies, waits for them, and re-layouts: 40.2 us -> none  [the longest x4 34.3 us: tri_update(): sides_chan = lax.all_to_all(sides, 'dap', 1, 2, tiled=True)]
  transfers between devices with their start and end apart: 8 -> 0, of which waited for: 8 -> 0; matrix products, arithmetic and copies ran while one was open for 27% -> 0% of each run, Pallas kernels for 0% -> 0%
where the time goes in v2:
time: 787 us; the launch traced here: 778 us
  Pallas kernels  765 us (97%)
  local copies, waits for them, and re-layouts  11.9 us (2%)
    pallas_call x10, Pallas kernels, call(): pl.pallas_call(kernel, grid=grid, out_shape=tuple(outs), in_specs=in_spec...  765 us

profile of v2, /device:TPU:97, one launch (start us, length us, event | category | flops | bytes accessed | tf_op | source)
XLA Modules:
  0.0 778.4 jit_solution(11863711843807787594)
XLA Ops:
  0.6 0.7 convert_element_type.6
  1.3 0.6 slice_bitcast_fusion.7
  1.9 0.8 broadcast_in_dim.25.refs_2_
  2.7 1.1 copy.13
  3.8 0.7 slice_bitcast_fusion
  4.5 18.4 %project.2.refs_4_.refs_0_.refs_6_ = bf16[4,2,2,2,2,2,2,24,768]{8,7,6,5,4,3,2,1,0:T(8,128)(2,1)} custom-call(bf16[24,768,128]{2,1,0:T(8,128)(2,1)} %refs_0_.6, s32[24,768]{1,0:T(8,128)} %refs_1_.6, f32[2,128,128]{2,1,0:T(8,128)} %broadcast_in_dim.25.refs_2_, bf16[512,128]{1,0:T(8,128)(2,1)} %get-tuple-element.38.refs_3_), custom_call_target="tpu_custom_call" | custom-call | tf_op jit(solution)/shard_map/project/pallas_call | solution.py:363
  22.9 129.0 %project.3 = (bf16[4,2,2,2,2,2,2,24,768]{8,7,6,5,4,3,2,1,0:T(8,128)(2,1)}, bf16[4,2,5,2,2,2,2,2,24,768]{9,8,7,6,5,4,3,2,1,0:T(8,128)(2,1)}) custom-call(bf16[24,768,128]{2,1,0:T(8,128)(2,1)} %refs_0_.7, s32[24,768]{1,0:T(8,128)} %refs_1_.7, f32[2,128,128]{2,1,0:T(8,128)} %broadcast_in_dim.25.refs_2_, bf16[512,128]{1,0:T(8,128)(2,1)} %get-tuple-element.38.refs_3_, ...), custom_call_target="tpu_custom_call" | custom-call | tf_op jit(solution)/shard_map/project/pallas_call | solution.py:363
  151.9 115.5 %triangle.4 = (bf16[4,1,2,2,2,2,2,24,768]{8,7,6,5,4,3,2,1,0:T(8,128)(2,1)}, bf16[4,2,5,2,2,2,2,2,24,768]{9,8,7,6,5,4,3,2,1,0:T(8,128)(2,1)}) custom-call(bf16[4,2,2,2,2,2,2,24,768]{8,7,6,5,4,3,2,1,0:T(8,128)(2,1)} %project.2.refs_4_.refs_0_.refs_6_, ...), custom_call_target="tpu_custom_call" | custom-call | tf_op jit(solution)/shard_map/triangle/pallas_call | solution.py:363
  267.3 0.0 copy-start
  267.4 0.0 copy-start.1
  267.4 0.0 copy-start.2
  267.4 0.0 copy-start.4
  267.4 65.9 %triangle.5 = (bf16[4,1,2,2,2,2,2,24,768]{8,7,6,5,4,3,2,1,0:T(8,128)(2,1)}, bf16[4,1,5,2,2,2,2,2,24,768]{9,8,7,6,5,4,3,2,1,0:T(8,128)(2,1)}) custom-call(bf16[4,2,2,2,2,2,2,24,768]{8,7,6,5,4,3,2,1,0:T(8,128)(2,1)} %get-tuple-element.21.refs_12_.refs_0_.refs_6_, ...), custom_call_target="tpu_custom_call" | custom-call | tf_op jit(solution)/shard_map/triangle/pallas_call | solution.py:363
  333.3 0.0 copy-done
  333.3 0.1 copy.11
  333.4 0.0 copy-done.1
  333.4 0.1 copy.12
  333.6 0.7 slice_bitcast_fusion.2
  334.2 0.0 copy-done.2
  334.2 0.8 broadcast_in_dim.29.refs_6_.refs_1_
  335.0 0.0 copy-done.4
  335.0 0.6 slice_bitcast_fusion.6
  335.5 0.8 broadcast_in_dim.27.refs_3_
  336.3 65.6 %finish_project.2 = (bf16[24,128,768]{2,1,0:T(8,128)(2,1)}, bf16[4,2,2,2,2,2,2,24,768]{8,7,6,5,4,3,2,1,0:T(8,128)(2,1)}, bf16[4,1,5,2,2,2,2,2,24,768]{9,8,7,6,5,4,3,2,1,0:T(8,128)(2,1)}) custom-call(bf16[24,768,128]{2,1,0:T(8,128)(2,1)} %refs_0_.6, s32[24,768]{1,0:T(8,128)} %refs_1_.6, f32[2,128,128]{2,1,0:T(8,128)} %broadcast_in_dim.25.refs_2_, ...), custom_call_target="tpu_custom_call" | custom-call | tf_op jit(solution)/shard_map/finish_project/pallas_call | solution.py:363
  401.9 114.7 %finish_project.3 = (bf16[24,128,768]{2,1,0:T(8,128)(2,1)}, bf16[4,2,2,2,2,2,2,24,768]{8,7,6,5,4,3,2,1,0:T(8,128)(2,1)}, bf16[4,2,5,2,2,2,2,2,24,768]{9,8,7,6,5,4,3,2,1,0:T(8,128)(2,1)}) custom-call(bf16[24,768,128]{2,1,0:T(8,128)(2,1)} %refs_0_.7, s32[24,768]{1,0:T(8,128)} %refs_1_.7, f32[2,128,128]{2,1,0:T(8,128)} %broadcast_in_dim.25.refs_2_, ...), custom_call_target="tpu_custom_call" | custom-call | tf_op jit(solution)/shard_map/finish_project/pallas_call | solution.py:363
  516.5 114.1 %triangle.6 = (bf16[4,1,2,2,2,2,2,24,768]{8,7,6,5,4,3,2,1,0:T(8,128)(2,1)}, bf16[4,2,5,2,2,2,2,2,24,768]{9,8,7,6,5,4,3,2,1,0:T(8,128)(2,1)}) custom-call(bf16[4,2,2,2,2,2,2,24,768]{8,7,6,5,4,3,2,1,0:T(8,128)(2,1)} %get-tuple-element.27.refs_14_.refs_0_.refs_6_, ...), custom_call_target="tpu_custom_call" | custom-call | tf_op jit(solution)/shard_map/triangle/pallas_call | solution.py:363
  630.7 0.0 copy-start.3
  630.7 63.4 %triangle.7 = (bf16[4,1,2,2,2,2,2,24,768]{8,7,6,5,4,3,2,1,0:T(8,128)(2,1)}, bf16[4,1,5,2,2,2,2,2,24,768]{9,8,7,6,5,4,3,2,1,0:T(8,128)(2,1)}) custom-call(bf16[4,2,2,2,2,2,2,24,768]{8,7,6,5,4,3,2,1,0:T(8,128)(2,1)} %get-tuple-element.30.refs_12_.refs_0_.refs_6_, ...), custom_call_target="tpu_custom_call" | custom-call | tf_op jit(solution)/shard_map/triangle/pallas_call | solution.py:363
  694.1 0.0 copy-done.3
  694.1 0.8 broadcast_in_dim.31.refs_2_
  694.8 61.6 %finish.2 = (bf16[24,768,128]{2,1,0:T(8,128)(2,1)}, bf16[4,1,5,2,2,2,2,2,24,768]{9,8,7,6,5,4,3,2,1,0:T(8,128)(2,1)}) custom-call(bf16[24,128,768]{2,1,0:T(8,128)(2,1)} %get-tuple-element.26.refs_0_, f32[2,128,128]{2,1,0:T(8,128)} %broadcast_in_dim.29.refs_6_.refs_1_, f32[2,128,128]{2,1,0:T(8,128)} %broadcast_in_dim.31.refs_2_, ...), custom_call_target="tpu_custom_call" | custom-call | tf_op jit(solution)/shard_map/finish/pallas_call | solution.py:363
  756.5 16.5 %finish.3 = bf16[24,768,128]{2,1,0:T(8,128)(2,1)} custom-call(bf16[24,128,768]{2,1,0:T(8,128)(2,1)} %get-tuple-element.36.refs_0_, f32[2,128,128]{2,1,0:T(8,128)} %broadcast_in_dim.29.refs_6_.refs_1_, f32[2,128,128]{2,1,0:T(8,128)} %broadcast_in_dim.31.refs_2_, bf16[128,128]{1,0:T(8,128)(2,1)} %get-tuple-element.49.refs_3_, ...), custom_call_target="tpu_custom_call" | custom-call | tf_op jit(solution)/shard_map/finish/pallas_call | solution.py:363
  772.9 5.0 copy.15
  (1 shorter events, 0.0 us)
Async XLA Ops:
  267.3 65.9 %copy-start = (bf16[2,128,128]{2,1,0:T(8,128)(2,1)S(1)}, bf16[2,128,128]{2,1,0:T(8,128)(2,1)}, u32[]{:S(2)}) copy-start(bf16[2,128,128]{2,1,0:T(8,128)(2,1)} %param.15) | copy-start | bytes 196612
  267.4 66.1 %copy-start.1 = (bf16[2,128,128]{2,1,0:T(8,128)(2,1)S(1)}, bf16[2,128,128]{2,1,0:T(8,128)(2,1)}, u32[]{:S(2)}) copy-start(bf16[2,128,128]{2,1,0:T(8,128)(2,1)} %param.17) | copy-start | bytes 196612
  267.4 66.9 %copy-start.2 = (f32[2,128]{1,0:T(2,128)S(1)}, f32[2,128]{1,0:T(2,128)}, u32[]{:S(2)}) copy-start(f32[2,128]{1,0:T(2,128)} %get-tuple-element.46) | copy-start | bytes 3076
  267.4 67.6 %copy-start.4 = (bf16[2,2,128]{2,1,0:T(2,128)(2,1)S(1)}, bf16[2,2,128]{2,1,0:T(2,128)(2,1)}, u32[]{:S(2)}) copy-start(bf16[2,2,128]{2,1,0:T(2,128)(2,1)} %param.16) | copy-start | bytes 3076
  630.7 63.4 %copy-start.3 = (f32[2,128]{1,0:T(2,128)S(1)}, f32[2,128]{1,0:T(2,128)}, u32[]{:S(2)}) copy-start(f32[2,128]{1,0:T(2,128)} %get-tuple-element.44) | copy-start | bytes 3076

commit v3 on v2

--- a/solution.py
+++ b/solution.py
@@ -25,60 +25,81 @@
     return lax.dot_general(a, b, (((1,), (0,)), ((), ())), preferred_element_type=F32)
 
 
-def _project(z_t, norm_ref, wp_ref, scr, r, kk):
+def _lane(kk):
+    return slice(kk * LANES, (kk + 1) * LANES)
+
+
+def _wide(v, width):
+    return jnp.concatenate([v] * (width // LANES), axis=1)
+
+
+def _project(z_t, norm_ref, wp_ref, scr, r):
     hid = wp_ref.shape[0] // 4
-    x_t = _norm_cols(z_t, norm_ref[0], norm_ref[1])
+    width = z_t.shape[1]
+    x_t = _norm_cols(z_t, _wide(norm_ref[0], width), _wide(norm_ref[1], width))
     q = _mm(wp_ref[...], x_t)
     for s in range(2):
         p, g = q[2 * s * hid:(2 * s + 1) * hid], q[(2 * s + 1) * hid:(2 * s + 2) * hid]
-        scr[kk, pl.ds(s * hid * RB + r, hid, stride=RB), :] = jax.nn.sigmoid(g) * p
-
-
-def _emit_sides(scr, m_ref, out_ref, kk, topo):
+        v = jax.nn.sigmoid(g) * p
+        for kk in range(width // LANES):
+            scr[kk, pl.ds(s * hid * RB + r, hid, stride=RB), :] = v[:, _lane(kk)]
+
+
+def _each_tile(width, f):
+    def body(kk, c):
+        f(kk, pl.ds(pl.multiple_of(kk * LANES, LANES), LANES))
+        return c
+    lax.fori_loop(0, width // LANES, body, 0)
+
+
+def _emit_sides(scr, m_ref, out_ref, topo):
     half = scr.shape[1] // 2
-    lanes = slice(kk * LANES, (kk + 1) * LANES)
-    keep = m_ref[:, lanes].astype(F32)
-    for q in range(topo.nq):
-        for rho, owner in topo.blocks(q):
+
+    def tile(kk, lanes):
+        keep = m_ref[:, lanes].astype(F32)
+        for q in range(topo.nq):
             for s in range(2):
-                at = pl.multiple_of(s * half + (owner * topo.nq + q) * RB, RB)
-                out_ref[(q, s) + rho + (slice(None), lanes)] = (scr[kk, pl.ds(at, RB), :] * keep).astype(BF16)
-
-
-def _finish(z_t, r, kk, scr_y, norm_ref, mid_ref, wg_ref, wo_ref):
+                for rho, owner in topo.blocks(topo.order(q, s)):
+                    at = pl.multiple_of(s * half + (owner * topo.nq + q) * RB, RB)
+                    out_ref[(q, s) + rho + (slice(None), lanes)] = (scr[kk, pl.ds(at, RB), :] * keep).astype(BF16)
+    _each_tile(m_ref.shape[1], tile)
+
+
+def _finish(z_t, r, scr_y, norm_ref, mid_ref, wg_ref, wo_ref):
     hid = wo_ref.shape[1]
-    x_t = _norm_cols(z_t, norm_ref[0], norm_ref[1])
+    width = z_t.shape[1]
+    x_t = _norm_cols(z_t, _wide(norm_ref[0], width), _wide(norm_ref[1], width))
     gate = jax.nn.sigmoid(_mm(wg_ref[...], x_t))
-    y = scr_y[kk, pl.ds(r, hid, stride=RB), :]
-    y = (y * mid_ref[0] + mid_ref[1]).astype(BF16)
+    y = [scr_y[kk, pl.ds(r, hid, stride=RB), :] for kk in range(width // LANES)]
+    y = jnp.concatenate([(v * mid_ref[0] + mid_ref[1]).astype(BF16) for v in y], axis=1)
     return (z_t + gate * _mm(wo_ref[...], y)).astype(BF16)
 
 
-def _norm_mid(t_refs, scr_y, kk, topo):
-    lanes = slice(kk * LANES, (kk + 1) * LANES)
-    tiles = [(q,) + rest for q in range(topo.nq) for rest in topo.landed(q)]
+def _norm_mid(t_refs, scr_y, topo):
+    tiles = [(q,) + rest for q in range(topo.nq) for rest in topo.landed(topo.order(q, 0))]
     inv_n = 1.0 / len(tiles)
 
-    def load(tile):
-        return t_refs[tile[1]][(tile[0],) + tile[2] + (slice(None), lanes)].astype(F32)
-
-    def total(f):
-        part = [f(load(t)) for t in tiles[:4]]
-        for i, t in enumerate(tiles[4:]):
-            part[i % 4] = part[i % 4] + f(load(t))
-        return (part[0] + part[1]) + (part[2] + part[3])
-    mean = total(lambda v: v) * inv_n
-    inv = lax.rsqrt(total(lambda v: (v - mean) * (v - mean)) * inv_n + 1e-5)
-    for t in tiles:
-        at = pl.multiple_of((t[3] * topo.nq + t[0]) * RB, RB)
-        scr_y[kk, pl.ds(at, RB), :] = (load(t) - mean) * inv
-
-
-def _row_loop(width, f):
+    def tile(kk, lanes):
+        def load(t):
+            return t_refs[t[1]][(t[0],) + t[2] + (slice(None), lanes)].astype(F32)
+
+        def total(f):
+            part = [f(load(t)) for t in tiles[:4]]
+            for i, t in enumerate(tiles[4:]):
+                part[i % 4] = part[i % 4] + f(load(t))
+            return (part[0] + part[1]) + (part[2] + part[3])
+        mean = total(lambda v: v) * inv_n
+        inv = lax.rsqrt(total(lambda v: (v - mean) * (v - mean)) * inv_n + 1e-5)
+        for t in tiles:
+            at = pl.multiple_of((t[3] * topo.nq + t[0]) * RB, RB)
+            scr_y[kk, pl.ds(at, RB), :] = (load(t) - mean) * inv
+    _each_tile(scr_y.shape[0] * LANES, tile)
+
+
+def _row_loop(f):
     def body(i, c):
         for u in range(UNROLL):
-            for kk in range(width // LANES):
-                f(i * UNROLL + u, kk, slice(kk * LANES, (kk + 1) * LANES))
+            f(i * UNROLL + u)
         return c
     lax.fori_loop(0, RB // UNROLL, body, 0)
 
@@ -89,11 +110,14 @@
         ring = self.side.bit_length() - 1
         self.nq = 2 * ring
         self.nb = self.nq + 1
-        links = [(axis, bit) for bit in range(ring) for axis in ("x", "y")]
-        self.order = [[("core", 0)] + [links[(q + i) % self.nq] for i in range(self.nq)] for q in range(self.nq)]
+        self.links = [(axis, bit) for bit in range(ring) for axis in ("x", "y")]
         self.weight = {("core", 0): 1}
         self.weight.update({("x", b): 2 << b for b in range(ring)})
         self.weight.update({("y", b): (2 << ring) << b for b in range(ring)})
+
+    def order(self, q, core_first):
+        links = [self.links[(q + i) % self.nq] for i in range(self.nq)]
+        return [("core", 0)] + links if core_first else links + [("core", 0)]
 
     def here(self):
         me = lax.axis_index("dap")
@@ -104,24 +128,31 @@
             self.bit[axis, b] = lax.rem(v // (1 << b) + v // (2 << b), 2) if axis != "core" else v
         return self
 
-    def partner(self, link):
+    def neighbour(self, link):
         axis, b = link
         pos = dict(self.pos)
         v, span = pos[axis], 2 << b
-        base = v - lax.rem(v, span)
-        pos[axis] = base + (span - 1) - lax.rem(v, span)
+        pos[axis] = v - lax.rem(v, span) + (span - 1) - lax.rem(v, span)
         return (pos["y"] * self.side + pos["x"]) * 2 + pos["core"]
 
-    def blocks(self, q):
+    def partner(self, q, core_first, s):
+        at = s - 1 if core_first else s
+        if at < 0 or at >= self.nq:
+            return self.neighbour(("core", 0))
+        i = lax.rem(q + at, self.nq)
+        hit = [jnp.where(i == k, self.neighbour(link), 0) for k, link in enumerate(self.links)]
+        return functools.reduce(lambda u, v: u + v, hit)
+
+    def blocks(self, order):
         out = [((), 0)]
-        for link in self.order[q]:
+        for link in order:
             w, own = self.weight[link], self.bit[link]
             out = [(r + (f,), o + w * (1 - own if f else own)) for r, o in out for f in (0, 1)]
         return out
 
-    def landed(self, q):
+    def landed(self, order):
         out = []
-        for rho, owner in self.blocks(q):
+        for rho, owner in self.blocks(order):
             last = max([i for i, f in enumerate(rho) if f], default=-1)
             idx = (0,) * self.nb if last < 0 else rho[:last] + (0,) * (self.nb - last)
             out.append((last + 1, idx, owner))
@@ -144,9 +175,9 @@
         pos = {"core": p % 2, "x": p // 2 % self.side, "y": p // 2 // self.side}
         return {k: (pos[k[0]] if k[0] == "core" else (pos[k[0]] >> k[1] ^ pos[k[0]] >> (k[1] + 1)) & 1) for k in self.weight}
 
-    def relative(self, q, p):
+    def relative(self, order, p):
         bits = self.gray_bits(p)
-        return tuple((1 - self.bit[k]) if bits[k] else self.bit[k] for k in self.order[q])
+        return tuple((1 - self.bit[k]) if bits[k] else self.bit[k] for k in order)
 
 
 class Exchange:
@@ -160,15 +191,25 @@
         w = self.src.shape[-1] // 2
         return 0, (slice(None), pl.ds(sub * w, w))
 
+    def _first(self, sub):
+        return sub == 1 and not self.cut
+
     def _copy(self, q, sub, s, a, b):
         return pltpu.make_async_remote_copy(
             src_ref=a, dst_ref=b, send_sem=self.ssem.at[q, sub, s], recv_sem=self.rsem.at[q, sub, s],
-            device_id={"dap": self.topo.partner(self.topo.order[q][s])}, device_id_type=pl.DeviceIdType.MESH)
+            device_id={"dap": self.topo.partner(q, self._first(sub), s)}, device_id_type=pl.DeviceIdType.MESH)
+
+    def _streams(self, f):
+        def body(q, c):
+            f(q)
+            return c
+        lax.fori_loop(0, self.topo.nq, body, 0)
 
     def start(self, sub, s):
         nb, free = self.topo.nb, (slice(None),)
         k, tail = self._tail(sub)
-        for q in range(self.topo.nq):
+
+        def stream(q):
             for t in range(-1, s):
                 if t < 0:
                     idx = (0,) * s + (1,) + free * (nb - 1 - s) + tail
@@ -177,6 +218,7 @@
                     idx = free * t + (1,) + (0,) * (s - 1 - t) + (1,) + free * (nb - 1 - s) + tail
                     a = self.dst.at[(q, k, t) + idx]
                 self._copy(q, sub, s, a, self.dst.at[(q, k, s) + idx]).start()
+        self._streams(stream)
 
     def _whole(self, q, sub, s):
         k, tail = self._tail(sub)
@@ -184,65 +226,56 @@
         return self._copy(q, sub, s, ref, ref)
 
     def arrive(self, sub, s):
-        for q in range(self.topo.nq):
-            self._whole(q, sub, s).wait_recv()
+        self._streams(lambda q: self._whole(q, sub, s).wait_recv())
 
     def drain(self):
         for sub in range(2):
             for s in range(self.topo.nb):
-                for q in range(self.topo.nq):
-                    self._whole(q, sub, s).wait_send()
+                self._streams(lambda q, sub=sub, s=s: self._whole(q, sub, s).wait_send())
 
     def barrier(self):
         bar = pltpu.get_barrier_semaphore()
         for link in self.topo.weight:
-            pl.semaphore_signal(bar, inc=1, device_id={"dap": self.topo.partner(link)}, device_id_type=pl.DeviceIdType.MESH)
+            pl.semaphore_signal(bar, inc=1, device_id={"dap": self.topo.neighbour(link)}, device_id_type=pl.DeviceIdType.MESH)
         pl.semaphore_wait(bar, len(self.topo.weight))
 
     def moves(self):
         out = []
         for s in range(self.topo.nb):
-            for sub in range(2):
+            for sub in (range(2) if self.cut else (1, 0)):
                 def move(s=s, sub=sub):
                     self.arrive(sub, s)
                     if s + 1 < self.topo.nb:
                         self.start(sub, s + 1)
-                out.append(move)
+                out.append((2 * s + (sub + 1 if self.cut else 0.4 if sub and s == 0 else 1 - sub), move))
         return out
 
 
 def _project_kernel(topo, z_ref, m_ref, norm_ref, wp_ref, out_ref, scr):
-    def row(r, kk, lanes):
-        _project(z_ref[r, lanes, :].astype(F32).T, norm_ref, wp_ref, scr, r, kk)
-    _row_loop(z_ref.shape[1], row)
-    for kk in range(z_ref.shape[1] // LANES):
-        _emit_sides(scr, m_ref, out_ref, kk, topo)
+    _row_loop(lambda r: _project(z_ref[r].astype(F32).T, norm_ref, wp_ref, scr, r))
+    _emit_sides(scr, m_ref, out_ref, topo)
 
 
 def _finish_project_kernel(topo, z_ref, m_ref, n0_ref, mid_ref, wg_ref, wo_ref, n1_ref, wp_ref, *refs):
     t_refs, (zt_ref, out_ref, scr_y, scr) = refs[:-4], refs[-4:]
-    for kk in range(z_ref.shape[1] // LANES):
-        _norm_mid(t_refs, scr_y, kk, topo)
-
-    def row(r, kk, lanes):
-        z_t = z_ref[r, lanes, :].astype(F32).T
-        z_new = _finish(z_t, r, kk, scr_y, n0_ref, mid_ref, wg_ref, wo_ref)
-        zt_ref[r, :, lanes] = z_new
-        _project(z_new.astype(F32), n1_ref, wp_ref, scr, r, kk)
-    _row_loop(z_ref.shape[1], row)
-    for kk in range(z_ref.shape[1] // LANES):
-        _emit_sides(scr, m_ref, out_ref, kk, topo)
+    _norm_mid(t_refs, scr_y, topo)
+
+    def row(r):
+        z_new = _finish(z_ref[r].astype(F32).T, r, scr_y, n0_ref, mid_ref, wg_ref, wo_ref)
+        zt_ref[r] = z_new
+        _project(z_new.astype(F32), n1_ref, wp_ref, scr, r)
+    _row_loop(row)
+    _emit_sides(scr, m_ref, out_ref, topo)
 
 
 def _finish_kernel(topo, zt_ref, n0_ref, mid_ref, wg_ref, wo_ref, *refs):
     t_refs, (z_ref, scr_y) = refs[:-2], refs[-2:]
-    for kk in range(z_ref.shape[1] // LANES):
-        _norm_mid(t_refs, scr_y, kk, topo)
-
-    def row(r, kk, lanes):
-        z_new = _finish(zt_ref[r, :, lanes].astype(F32), r, kk, scr_y, n0_ref, mid_ref, wg_ref, wo_ref)
-        z_ref[r, lanes, :] = z_new.astype(F32).T.astype(BF16)
-    _row_loop(z_ref.shape[1], row)
+    _norm_mid(t_refs, scr_y, topo)
+
+    def row(r):
+        z_new = _finish(zt_ref[r].astype(F32), r, scr_y, n0_ref, mid_ref, wg_ref, wo_ref)
+        z_ref[r] = z_new.astype(F32).T.astype(BF16)
+    _row_loop(row)
 
 
 def _triangle_kernel(topo, contract, *refs):
@@ -252,13 +285,17 @@
     step = pl.program_id(0)
 
     def gather(q):
-        for i, (piece, idx, owner) in enumerate(topo.landed(q)):
+        a_order, b_order = topo.order(q, 0), topo.order(q, 1)
+        rhos = [dict(zip(a_order, rho)) for rho, _ in topo.blocks(a_order)]
+        for i, (piece, idx, _) in enumerate(topo.landed(a_order)):
             a_scr[i] = a_refs[piece][(0,) + idx]
-            b_scr[topo.natural(owner) if contract else i] = b_refs[piece][(0,) + idx]
+        for (rho, owner), (piece, idx, _) in zip(topo.blocks(b_order), topo.landed(b_order)):
+            at = topo.natural(owner) if contract else rhos.index(dict(zip(b_order, rho)))
+            b_scr[at] = b_refs[piece][(0,) + idx]
 
     def scatter(q):
         for p in range(n):
-            out_ref[(0,) + topo.relative(q, p)] = a_scr[p]
+            out_ref[(0,) + topo.relative(topo.order(q, 0), p)] = a_scr[p]
     for q in range(topo.nq):
         pl.when(step == q)(functools.partial(gather, q))
     a, b = a_scr[...].reshape(n * rows, width), b_scr[...].reshape(n * rows, width)
@@ -346,16 +383,16 @@
             for sub in range(2):
                 ex.start(sub, 0)
         moves = ex.moves()
-        due = [max(1, int((i + 1) * pace)) if pace else steps for i in range(len(moves))]
+        due = [(max(1, round(t * pace)) if pace else steps, m) for t, m in moves]
         for g in range(1, steps):
-            now = [m for m, d in zip(moves, due) if d == g]
+            now = [m for d, m in due if d == g]
             if now:
                 pl.when(step == g)(lambda now=now: [m() for m in now] and None)
         body(topo, *work)
 
         @pl.when(step == steps - 1)
         def _():
-            for m, d in zip(moves, due):
+            for d, m in due:
                 if d >= steps:
                     m()
             ex.drain()
@@ -408,16 +445,16 @@
         zs, ms = (z_one, z_two), (mask_one, mask_two)
         mask_a, mask_b = ms
         s1, = project(sh, zs[0], mask_a, nin[0], wp[0])
-        s2, w1 = project(sh, zs[1], mask_b, nin[0], wp[0], moving=s1, cid=0)
+        s2, w1 = project(sh, zs[1], mask_b, nin[0], wp[0], moving=s1, cid=0, pace=5.5)
         t1, w2 = triangle(sh, (s1, w1), 1, moving=s2, cid=1)
         t2, v1 = triangle(sh, (s2, w2), 1, moving=t1, cid=2)
         flat = (nin[0], mid[0], wg[0], wo[0], nin[1], wp[1])
-        zt1, s1, v2 = finish_project(sh, zs[0], mask_a, *flat, (t1, v1), moving=t2, cid=3, pace=0.85)
-        zt2, s2, w1 = finish_project(sh, zs[1], mask_b, *flat, (t2, v2), moving=s1, cid=4, pace=1.9)
+        zt1, s1, v2 = finish_project(sh, zs[0], mask_a, *flat, (t1, v1), moving=t2, cid=3, pace=1.6)
+        zt2, s2, w1 = finish_project(sh, zs[1], mask_b, *flat, (t2, v2), moving=s1, cid=4, pace=3.2)
         t1, w2 = triangle(sh, (s1, w1), 0, moving=s2, cid=5)
         t2, v1 = triangle(sh, (s2, w2), 0, moving=t1, cid=6)
         flat = (nin[1], mid[1], wg[1], wo[1])
-        z1, v2 = finish(sh, zt1, *flat, (t1, v1), moving=t2, cid=7, pace=1.9)
+        z1, v2 = finish(sh, zt1, *flat, (t1, v1), moving=t2, cid=7, pace=3.4)
         z2, = finish(sh, zt2, *flat, (t2, v2))
         return z1, z2
 

time: 787 us -> 734 us (0.933); the launches traced: 778 us -> 734 us
  Pallas kernels: 765 us -> 720 us
    pallas_call x10, Pallas kernels: 765 us -> 720 us  [call(): pl.pallas_call(kernel, grid=grid, out_shape=tuple(outs), in_specs=in_spec...]
where the time goes in v3:
time: 734 us
  Pallas kernels  720 us (98%)
  local copies, waits for them, and re-layouts  11.9 us (2%)
    pallas_call x10, Pallas kernels, call(): pl.pallas_call(kernel, grid=grid, out_shape=tuple(outs), in_specs=in_spec...  720 us

profile of v3, /device:TPU:97, one launch (start us, length us, event | category | flops | bytes accessed | tf_op | source)
XLA Modules:
  0.0 733.7 jit_solution(14723628989400039231)
XLA Ops:
  0.6 0.7 convert_element_type.6
  1.3 0.6 slice_bitcast_fusion.7
  1.9 0.8 broadcast_in_dim.25.refs_2_
  2.7 1.1 copy.13
  3.8 0.7 slice_bitcast_fusion
  4.5 21.8 %project.2.refs_4_.refs_0_.refs_6_ = bf16[4,2,2,2,2,2,2,24,768]{8,7,6,5,4,3,2,1,0:T(8,128)(2,1)} custom-call(bf16[24,768,128]{2,1,0:T(8,128)(2,1)} %refs_0_.6, s32[24,768]{1,0:T(8,128)} %refs_1_.6, f32[2,128,128]{2,1,0:T(8,128)} %broadcast_in_dim.25.refs_2_, bf16[512,128]{1,0:T(8,128)(2,1)} %get-tuple-element.38.refs_3_), custom_call_target="tpu_custom_call" | custom-call | tf_op jit(solution)/shard_map/project/pallas_call | solution.py:400
  26.3 112.7 %project.3 = (bf16[4,2,2,2,2,2,2,24,768]{8,7,6,5,4,3,2,1,0:T(8,128)(2,1)}, bf16[4,2,5,2,2,2,2,2,24,768]{9,8,7,6,5,4,3,2,1,0:T(8,128)(2,1)}) custom-call(bf16[24,768,128]{2,1,0:T(8,128)(2,1)} %refs_0_.7, s32[24,768]{1,0:T(8,128)} %refs_1_.7, f32[2,128,128]{2,1,0:T(8,128)} %broadcast_in_dim.25.refs_2_, bf16[512,128]{1,0:T(8,128)(2,1)} %get-tuple-element.38.refs_3_, ...), custom_call_target="tpu_custom_call" | custom-call | tf_op jit(solution)/shard_map/project/pallas_call | solution.py:400
  139.0 107.1 %triangle.4 = (bf16[4,1,2,2,2,2,2,24,768]{8,7,6,5,4,3,2,1,0:T(8,128)(2,1)}, bf16[4,2,5,2,2,2,2,2,24,768]{9,8,7,6,5,4,3,2,1,0:T(8,128)(2,1)}) custom-call(bf16[4,2,2,2,2,2,2,24,768]{8,7,6,5,4,3,2,1,0:T(8,128)(2,1)} %project.2.refs_4_.refs_0_.refs_6_, ...), custom_call_target="tpu_custom_call" | custom-call | tf_op jit(solution)/shard_map/triangle/pallas_call | solution.py:400
  246.1 0.0 copy-start
  246.1 0.0 copy-start.1
  246.1 0.0 copy-start.2
  246.1 0.0 copy-start.4
  246.1 61.9 %triangle.5 = (bf16[4,1,2,2,2,2,2,24,768]{8,7,6,5,4,3,2,1,0:T(8,128)(2,1)}, bf16[4,1,5,2,2,2,2,2,24,768]{9,8,7,6,5,4,3,2,1,0:T(8,128)(2,1)}) custom-call(bf16[4,2,2,2,2,2,2,24,768]{8,7,6,5,4,3,2,1,0:T(8,128)(2,1)} %get-tuple-element.21.refs_12_.refs_0_.refs_6_, ...), custom_call_target="tpu_custom_call" | custom-call | tf_op jit(solution)/shard_map/triangle/pallas_call | solution.py:400
  308.0 0.0 copy-done
  308.0 0.1 copy.11
  308.1 0.0 copy-done.1
  308.2 0.1 copy.12
  308.3 0.7 slice_bitcast_fusion.2
  308.9 0.0 copy-done.2
  308.9 0.8 broadcast_in_dim.29.refs_6_.refs_1_
  309.7 0.0 copy-done.4
  309.7 0.6 slice_bitcast_fusion.6
  310.3 0.8 broadcast_in_dim.27.refs_3_
  311.0 60.9 %finish_project.2 = (bf16[24,128,768]{2,1,0:T(8,128)(2,1)}, bf16[4,2,2,2,2,2,2,24,768]{8,7,6,5,4,3,2,1,0:T(8,128)(2,1)}, bf16[4,1,5,2,2,2,2,2,24,768]{9,8,7,6,5,4,3,2,1,0:T(8,128)(2,1)}) custom-call(bf16[24,768,128]{2,1,0:T(8,128)(2,1)} %refs_0_.6, s32[24,768]{1,0:T(8,128)} %refs_1_.6, f32[2,128,128]{2,1,0:T(8,128)} %broadcast_in_dim.25.refs_2_, ...), custom_call_target="tpu_custom_call" | custom-call | tf_op jit(solution)/shard_map/finish_project/pallas_call | solution.py:400
  371.9 108.8 %finish_project.3 = (bf16[24,128,768]{2,1,0:T(8,128)(2,1)}, bf16[4,2,2,2,2,2,2,24,768]{8,7,6,5,4,3,2,1,0:T(8,128)(2,1)}, bf16[4,2,5,2,2,2,2,2,24,768]{9,8,7,6,5,4,3,2,1,0:T(8,128)(2,1)}) custom-call(bf16[24,768,128]{2,1,0:T(8,128)(2,1)} %refs_0_.7, s32[24,768]{1,0:T(8,128)} %refs_1_.7, f32[2,128,128]{2,1,0:T(8,128)} %broadcast_in_dim.25.refs_2_, ...), custom_call_target="tpu_custom_call" | custom-call | tf_op jit(solution)/shard_map/finish_project/pallas_call | solution.py:400
  480.8 107.8 %triangle.6 = (bf16[4,1,2,2,2,2,2,24,768]{8,7,6,5,4,3,2,1,0:T(8,128)(2,1)}, bf16[4,2,5,2,2,2,2,2,24,768]{9,8,7,6,5,4,3,2,1,0:T(8,128)(2,1)}) custom-call(bf16[4,2,2,2,2,2,2,24,768]{8,7,6,5,4,3,2,1,0:T(8,128)(2,1)} %get-tuple-element.27.refs_14_.refs_0_.refs_6_, ...), custom_call_target="tpu_custom_call" | custom-call | tf_op jit(solution)/shard_map/triangle/pallas_call | solution.py:400
  588.6 0.0 copy-start.3
  588.6 61.0 %triangle.7 = (bf16[4,1,2,2,2,2,2,24,768]{8,7,6,5,4,3,2,1,0:T(8,128)(2,1)}, bf16[4,1,5,2,2,2,2,2,24,768]{9,8,7,6,5,4,3,2,1,0:T(8,128)(2,1)}) custom-call(bf16[4,2,2,2,2,2,2,24,768]{8,7,6,5,4,3,2,1,0:T(8,128)(2,1)} %get-tuple-element.30.refs_12_.refs_0_.refs_6_, ...), custom_call_target="tpu_custom_call" | custom-call | tf_op jit(solution)/shard_map/triangle/pallas_call | solution.py:400
  649.6 0.0 copy-done.3
  649.6 0.8 broadcast_in_dim.31.refs_2_
  650.3 60.3 %finish.2 = (bf16[24,768,128]{2,1,0:T(8,128)(2,1)}, bf16[4,1,5,2,2,2,2,2,24,768]{9,8,7,6,5,4,3,2,1,0:T(8,128)(2,1)}) custom-call(bf16[24,128,768]{2,1,0:T(8,128)(2,1)} %get-tuple-element.26.refs_0_, f32[2,128,128]{2,1,0:T(8,128)} %broadcast_in_dim.29.refs_6_.refs_1_, f32[2,128,128]{2,1,0:T(8,128)} %broadcast_in_dim.31.refs_2_, ...), custom_call_target="tpu_custom_call" | custom-call | tf_op jit(solution)/shard_map/finish/pallas_call | solution.py:400
  710.6 18.1 %finish.3 = bf16[24,768,128]{2,1,0:T(8,128)(2,1)} custom-call(bf16[24,128,768]{2,1,0:T(8,128)(2,1)} %get-tuple-element.36.refs_0_, f32[2,128,128]{2,1,0:T(8,128)} %broadcast_in_dim.29.refs_6_.refs_1_, f32[2,128,128]{2,1,0:T(8,128)} %broadcast_in_dim.31.refs_2_, bf16[128,128]{1,0:T(8,128)(2,1)} %get-tuple-element.49.refs_3_, ...), custom_call_target="tpu_custom_call" | custom-call | tf_op jit(solution)/shard_map/finish/pallas_call | solution.py:400
  728.7 5.0 copy.15
  (1 shorter events, 0.0 us)
Async XLA Ops:
  246.1 61.9 %copy-start = (bf16[2,128,128]{2,1,0:T(8,128)(2,1)S(1)}, bf16[2,128,128]{2,1,0:T(8,128)(2,1)}, u32[]{:S(2)}) copy-start(bf16[2,128,128]{2,1,0:T(8,128)(2,1)} %param.15) | copy-start | bytes 196612
  246.1 62.0 %copy-start.1 = (bf16[2,128,128]{2,1,0:T(8,128)(2,1)S(1)}, bf16[2,128,128]{2,1,0:T(8,128)(2,1)}, u32[]{:S(2)}) copy-start(bf16[2,128,128]{2,1,0:T(8,128)(2,1)} %param.17) | copy-start | bytes 196612
  246.1 62.8 %copy-start.2 = (f32[2,128]{1,0:T(2,128)S(1)}, f32[2,128]{1,0:T(2,128)}, u32[]{:S(2)}) copy-start(f32[2,128]{1,0:T(2,128)} %get-tuple-element.46) | copy-start | bytes 3076
  246.1 63.6 %copy-start.4 = (bf16[2,2,128]{2,1,0:T(2,128)(2,1)S(1)}, bf16[2,2,128]{2,1,0:T(2,128)(2,1)}, u32[]{:S(2)}) copy-start(bf16[2,2,128]{2,1,0:T(2,128)(2,1)} %param.16) | copy-start | bytes 3076
  588.6 61.0 %copy-start.3 = (f32[2,128]{1,0:T(2,128)S(1)}, f32[2,128]{1,0:T(2,128)}, u32[]{:S(2)}) copy-start(f32[2,128]{1,0:T(2,128)} %get-tuple-element.44) | copy-start | bytes 3076

commit v4 on v3

--- a/solution.py
+++ b/solution.py
@@ -25,24 +25,12 @@
     return lax.dot_general(a, b, (((1,), (0,)), ((), ())), preferred_element_type=F32)
 
 
-def _lane(kk):
-    return slice(kk * LANES, (kk + 1) * LANES)
-
-
-def _wide(v, width):
-    return jnp.concatenate([v] * (width // LANES), axis=1)
-
-
-def _project(z_t, norm_ref, wp_ref, scr, r):
+def _project(z_t, norm_ref, wp_ref, scr, r, kk):
     hid = wp_ref.shape[0] // 4
-    width = z_t.shape[1]
-    x_t = _norm_cols(z_t, _wide(norm_ref[0], width), _wide(norm_ref[1], width))
-    q = _mm(wp_ref[...], x_t)
+    q = _mm(wp_ref[...], _norm_cols(z_t, norm_ref[0], norm_ref[1]))
     for s in range(2):
         p, g = q[2 * s * hid:(2 * s + 1) * hid], q[(2 * s + 1) * hid:(2 * s + 2) * hid]
-        v = jax.nn.sigmoid(g) * p
-        for kk in range(width // LANES):
-            scr[kk, pl.ds(s * hid * RB + r, hid, stride=RB), :] = v[:, _lane(kk)]
+        scr[kk, pl.ds(s * hid * RB + r, hid, stride=RB), :] = jax.nn.sigmoid(g) * p
 
 
 def _each_tile(width, f):
@@ -59,24 +47,22 @@
         keep = m_ref[:, lanes].astype(F32)
         for q in range(topo.nq):
             for s in range(2):
-                for rho, owner in topo.blocks(topo.order(q, s)):
+                for rho, owner in topo.blocks(topo.order(q)):
                     at = pl.multiple_of(s * half + (owner * topo.nq + q) * RB, RB)
                     out_ref[(q, s) + rho + (slice(None), lanes)] = (scr[kk, pl.ds(at, RB), :] * keep).astype(BF16)
     _each_tile(m_ref.shape[1], tile)
 
 
-def _finish(z_t, r, scr_y, norm_ref, mid_ref, wg_ref, wo_ref):
+def _finish(z_t, r, kk, scr_y, norm_ref, mid_ref, wg_ref, wo_ref):
     hid = wo_ref.shape[1]
-    width = z_t.shape[1]
-    x_t = _norm_cols(z_t, _wide(norm_ref[0], width), _wide(norm_ref[1], width))
-    gate = jax.nn.sigmoid(_mm(wg_ref[...], x_t))
-    y = [scr_y[kk, pl.ds(r, hid, stride=RB), :] for kk in range(width // LANES)]
-    y = jnp.concatenate([(v * mid_ref[0] + mid_ref[1]).astype(BF16) for v in y], axis=1)
+    gate = jax.nn.sigmoid(_mm(wg_ref[...], _norm_cols(z_t, norm_ref[0], norm_ref[1])))
+    y = scr_y[kk, pl.ds(r, hid, stride=RB), :]
+    y = (y * mid_ref[0] + mid_ref[1]).astype(BF16)
     return (z_t + gate * _mm(wo_ref[...], y)).astype(BF16)
 
 
 def _norm_mid(t_refs, scr_y, topo):
-    tiles = [(q,) + rest for q in range(topo.nq) for rest in topo.landed(topo.order(q, 0))]
+    tiles = [(q,) + rest for q in range(topo.nq) for rest in topo.landed(topo.order(q))]
     inv_n = 1.0 / len(tiles)
 
     def tile(kk, lanes):
@@ -96,10 +82,11 @@
     _each_tile(scr_y.shape[0] * LANES, tile)
 
 
-def _row_loop(f):
+def _row_loop(width, f):
     def body(i, c):
         for u in range(UNROLL):
-            f(i * UNROLL + u)
+            for kk in range(width // LANES):
+                f(i * UNROLL + u, kk, slice(kk * LANES, (kk + 1) * LANES))
         return c
     lax.fori_loop(0, RB // UNROLL, body, 0)
 
@@ -115,9 +102,9 @@
         self.weight.update({("x", b): 2 << b for b in range(ring)})
         self.weight.update({("y", b): (2 << ring) << b for b in range(ring)})
 
-    def order(self, q, core_first):
+    def order(self, q):
         links = [self.links[(q + i) % self.nq] for i in range(self.nq)]
-        return [("core", 0)] + links if core_first else links + [("core", 0)]
+        return links[:self.nq // 2] + [("core", 0)] + links[self.nq // 2:]
 
     def here(self):
         me = lax.axis_index("dap")
@@ -135,10 +122,10 @@
         pos[axis] = v - lax.rem(v, span) + (span - 1) - lax.rem(v, span)
         return (pos["y"] * self.side + pos["x"]) * 2 + pos["core"]
 
-    def partner(self, q, core_first, s):
-        at = s - 1 if core_first else s
-        if at < 0 or at >= self.nq:
+    def partner(self, q, s):
+        if s == self.nq // 2:
             return self.neighbour(("core", 0))
+        at = s if s < self.nq // 2 else s - 1
         i = lax.rem(q + at, self.nq)
         hit = [jnp.where(i == k, self.neighbour(link), 0) for k, link in enumerate(self.links)]
         return functools.reduce(lambda u, v: u + v, hit)
@@ -191,13 +178,10 @@
         w = self.src.shape[-1] // 2
         return 0, (slice(None), pl.ds(sub * w, w))
 
-    def _first(self, sub):
-        return sub == 1 and not self.cut
-
     def _copy(self, q, sub, s, a, b):
         return pltpu.make_async_remote_copy(
             src_ref=a, dst_ref=b, send_sem=self.ssem.at[q, sub, s], recv_sem=self.rsem.at[q, sub, s],
-            device_id={"dap": self.topo.partner(q, self._first(sub), s)}, device_id_type=pl.DeviceIdType.MESH)
+            device_id={"dap": self.topo.partner(q, s)}, device_id_type=pl.DeviceIdType.MESH)
 
     def _streams(self, f):
         def body(q, c):
@@ -240,42 +224,50 @@
         pl.semaphore_wait(bar, len(self.topo.weight))
 
     def moves(self):
-        out = []
+        mid, out = self.topo.nq // 2, []
         for s in range(self.topo.nb):
-            for sub in (range(2) if self.cut else (1, 0)):
+            for sub in range(2):
                 def move(s=s, sub=sub):
                     self.arrive(sub, s)
                     if s + 1 < self.topo.nb:
                         self.start(sub, s + 1)
-                out.append((2 * s + (sub + 1 if self.cut else 0.4 if sub and s == 0 else 1 - sub), move))
-        return out
-
-
-def _project_kernel(topo, z_ref, m_ref, norm_ref, wp_ref, out_ref, scr):
-    _row_loop(lambda r: _project(z_ref[r].astype(F32).T, norm_ref, wp_ref, scr, r))
+                out.append((2 * s + sub + 1 if s < mid else 2 * s + sub - 0.5 if s == mid else 2 * s + sub - 1, move))
+        return sorted(out, key=lambda m: m[0])
+
+
+def _project_kernel(topo, norm, wp, z_ref, m_ref, out_ref, scr):
+    def row(r, kk, lanes):
+        _project(z_ref[r, lanes, :].astype(F32).T, norm, wp, scr, r, kk)
+    _row_loop(z_ref.shape[1], row)
     _emit_sides(scr, m_ref, out_ref, topo)
 
 
-def _finish_project_kernel(topo, z_ref, m_ref, n0_ref, mid_ref, wg_ref, wo_ref, n1_ref, wp_ref, *refs):
+def _finish_project_kernel(topo, n0, mid, wg, wo, n1, wp, z_ref, m_ref, *refs):
     t_refs, (zt_ref, out_ref, scr_y, scr) = refs[:-4], refs[-4:]
     _norm_mid(t_refs, scr_y, topo)
 
-    def row(r):
-        z_new = _finish(z_ref[r].astype(F32).T, r, scr_y, n0_ref, mid_ref, wg_ref, wo_ref)
-        zt_ref[r] = z_new
-        _project(z_new.astype(F32), n1_ref, wp_ref, scr, r)
-    _row_loop(row)
+    def row(r, kk, lanes):
+        z_new = _finish(z_ref[r, lanes, :].astype(F32).T, r, kk, scr_y, n0, mid, wg, wo)
+        zt_ref[r, :, lanes] = z_new
+        _project(z_new.astype(F32), n1, wp, scr, r, kk)
+    _row_loop(z_ref.shape[1], row)
     _emit_sides(scr, m_ref, out_ref, topo)
 
 
-def _finish_kernel(topo, zt_ref, n0_ref, mid_ref, wg_ref, wo_ref, *refs):
+def _finish_kernel(topo, n0, mid, wg, wo, zt_ref, *refs):
     t_refs, (z_ref, scr_y) = refs[:-2], refs[-2:]
     _norm_mid(t_refs, scr_y, topo)
 
-    def row(r):
-        z_new = _finish(zt_ref[r].astype(F32), r, scr_y, n0_ref, mid_ref, wg_ref, wo_ref)
-        z_ref[r] = z_new.astype(F32).T.astype(BF16)
-    _row_loop(row)
+    def row(r, kk, lanes):
+        z_new = _finish(zt_ref[r, :, lanes].astype(F32), r, kk, scr_y, n0, mid, wg, wo)
+        z_ref[r, lanes, :] = z_new.astype(F32).T.astype(BF16)
+    _row_loop(z_ref.shape[1], row)
+
+
+def _finish_last_kernel(topo, n0, mid, wg, wo, zt_ref, other_ref, *refs):
+    t_refs, (z_ref, other_out, scr_y) = refs[:-3], refs[-3:]
+    other_out[...] = other_ref[...]
+    _finish_kernel(topo, n0, mid, wg, wo, zt_ref, *t_refs, z_ref, scr_y)
 
 
 def _triangle_kernel(topo, contract, *refs):
@@ -285,17 +277,13 @@
     step = pl.program_id(0)
 
     def gather(q):
-        a_order, b_order = topo.order(q, 0), topo.order(q, 1)
-        rhos = [dict(zip(a_order, rho)) for rho, _ in topo.blocks(a_order)]
-        for i, (piece, idx, _) in enumerate(topo.landed(a_order)):
+        for i, (piece, idx, owner) in enumerate(topo.landed(topo.order(q))):
             a_scr[i] = a_refs[piece][(0,) + idx]
-        for (rho, owner), (piece, idx, _) in zip(topo.blocks(b_order), topo.landed(b_order)):
-            at = topo.natural(owner) if contract else rhos.index(dict(zip(b_order, rho)))
-            b_scr[at] = b_refs[piece][(0,) + idx]
+            b_scr[topo.natural(owner) if contract else i] = b_refs[piece][(0,) + idx]
 
     def scatter(q):
         for p in range(n):
-            out_ref[(0,) + topo.relative(topo.order(q, 0), p)] = a_scr[p]
+            out_ref[(0,) + topo.relative(topo.order(q), p)] = a_scr[p]
     for q in range(topo.nq):
         pl.when(step == q)(functools.partial(gather, q))
     a, b = a_scr[...].reshape(n * rows, width), b_scr[...].reshape(n * rows, width)
@@ -329,6 +317,7 @@
         self.sides_spec = pl.BlockSpec((topo.nq, 2) + self.bits + (RB, self.kb), lambda i, j: (0, 0) + zero + (i, j))
         self.sides = jax.ShapeDtypeStruct((topo.nq, 2) + self.bits + (self.rows, self.width), BF16)
         self.tri = jax.ShapeDtypeStruct((topo.nq, 1) + self.bits + (self.rows, self.width), BF16)
+        self.z_out = jax.ShapeDtypeStruct(z.shape, BF16)
         self.zt = jax.ShapeDtypeStruct((self.rows, self.cz, self.width), BF16)
         self.scr = pltpu.VMEM((self.kb // LANES, 2 * self.hid * RB, LANES), F32)
         self.scr_y = pltpu.VMEM((self.kb // LANES, self.hid * RB, LANES), F32)
@@ -353,83 +342,98 @@
         return self._pieces(1, (self.rows, self.width), lambda g: ((g[0], side), (0, 0)))
 
 
-def call(sh, name, body, grid, ins, in_specs, outs, out_specs, scratch, moving=None, cid=0, pace=None):
+def _prepare(raw, ready, update):
+    if len(ready.shape) == 3:
+        for i in range(2):
+            row = raw[update, i:i + 1, :].astype(F32)
+            ready[i] = jnp.broadcast_to(row, (LANES, row.shape[1])).T
+    else:
+        ready[...] = raw[update].astype(F32).T.astype(BF16)
+
+
+def call(sh, name, body, grid, params, ins, in_specs, outs, out_specs, scratch, moving=None, cid=0, pace=None):
     topo = sh.topo
     steps = math.prod(grid)
-    params = dict(vmem_limit_bytes=62 * 1024 * 1024)
+    compiler = dict(vmem_limit_bytes=62 * 1024 * 1024)
     hbm = pl.BlockSpec(memory_space=pl.ANY)
-    n_in, n_out = len(ins), len(outs)
+    n_par, n_in, n_out = len(params), len(ins), len(outs)
+    ready = [pltpu.VMEM((2, p.shape[-1], LANES), F32) if p.shape[1] == 2 else pltpu.VMEM(p.shape[:0:-1], BF16) for p, _ in params]
+    ins, in_specs = [p for p, _ in params] + list(ins), [_whole(p) for p, _ in params] + list(in_specs)
+    scratch, sems = ready + list(scratch), []
     if moving is not None:
-        ins, in_specs = list(ins) + [moving], list(in_specs) + [hbm]
+        ins, in_specs = ins + [moving], in_specs + [hbm]
         outs, out_specs = list(outs) + [sh.landing(moving)], list(out_specs) + [hbm]
-        sems = pltpu.SemaphoreType.DMA((topo.nq, 2, topo.nb))
-        scratch = list(scratch) + [sems, sems]
-        params.update(collective_id=cid, has_side_effects=True)
+        sems = [pltpu.SemaphoreType.DMA((topo.nq, 2, topo.nb))] * 2
+        compiler.update(collective_id=cid, has_side_effects=True)
+    n_move = len(sems) // 2
 
     def kernel(*refs):
         topo.here()
-        if moving is None:
-            body(topo, *refs)
-            return
-        work = refs[:n_in] + refs[n_in + 1:n_in + 1 + n_out] + refs[n_in + n_out + 2:-2]
-        ex = Exchange(topo, refs[n_in], refs[n_in + 1 + n_out], refs[-2], refs[-1])
+        raw, refs = refs[:n_par], refs[n_par:]
+        work_in, refs = refs[:n_in], refs[n_in:]
+        src, refs = refs[:n_move], refs[n_move:]
+        work_out, refs = refs[:n_out], refs[n_out:]
+        dst, refs = refs[:n_move], refs[n_move:]
+        done, work_scr, sem_refs = refs[:n_par], refs[n_par:len(refs) - 2 * n_move], refs[len(refs) - 2 * n_move:]
         step = pl.program_id(0)
         for d, size in enumerate(grid[1:], 1):
             step = step * size + pl.program_id(d)
+        due = []
+        if n_move:
+            ex = Exchange(topo, src[0], dst[0], *sem_refs)
+            due = [(max(1, round(t * pace)) if pace else steps, m) for t, m in ex.moves()]
 
         @pl.when(step == 0)
         def _():
-            ex.barrier()
-            for sub in range(2):
-                ex.start(sub, 0)
-        moves = ex.moves()
-        due = [(max(1, round(t * pace)) if pace else steps, m) for t, m in moves]
+            if n_move:
+                ex.barrier()
+                for sub in range(2):
+                    ex.start(sub, 0)
+            for a, b, (_, update) in zip(raw, done, params):
+                _prepare(a, b, update)
         for g in range(1, steps):
             now = [m for d, m in due if d == g]
             if now:
                 pl.when(step == g)(lambda now=now: [m() for m in now] and None)
-        body(topo, *work)
-
-        @pl.when(step == steps - 1)
-        def _():
-            for d, m in due:
-                if d >= steps:
-                    m()
-            ex.drain()
+        body(topo, *done, *work_in, *work_out, *work_scr)
+        if n_move:
+            @pl.when(step == steps - 1)
+            def _():
+                for d, m in due:
+                    if d >= steps:
+                        m()
+                ex.drain()
 
     return pl.pallas_call(kernel, grid=grid, out_shape=tuple(outs), in_specs=in_specs, out_specs=tuple(out_specs),
-                          scratch_shapes=scratch, compiler_params=pltpu.CompilerParams(**params), name=name)(*ins)
-
-
-def project(sh, z, m, norm, wp, **move):
-    return call(sh, "project", _project_kernel, sh.grid, (z, m, norm, wp), [sh.z_spec, sh.m_spec, _whole(norm), _whole(wp)],
+                          scratch_shapes=scratch + sems, compiler_params=pltpu.CompilerParams(**compiler), name=name)(*ins)
+
+
+def project(sh, params, z, m, **move):
+    return call(sh, "project", _project_kernel, sh.grid, params, (z, m), [sh.z_spec, sh.m_spec],
                 [sh.sides], [sh.sides_spec], [sh.scr], **move)
 
 
-def finish_project(sh, z, m, n0, mid, wg, wo, n1, wp, t, **move):
-    flat = (n0, mid, wg, wo, n1, wp)
-    return call(sh, "finish_project", _finish_project_kernel, sh.grid, (z, m) + flat + (t[0],) + (t[1],) * sh.topo.nb,
-                [sh.z_spec, sh.m_spec] + [_whole(a) for a in flat] + sh.tri_pieces(),
-                [sh.zt, sh.sides], [sh.zt_spec, sh.sides_spec], [sh.scr_y, sh.scr], **move)
-
-
-def finish(sh, zt, n0, mid, wg, wo, t, **move):
-    flat = (n0, mid, wg, wo)
-    return call(sh, "finish", _finish_kernel, sh.grid, (zt,) + flat + (t[0],) + (t[1],) * sh.topo.nb,
-                [sh.zt_spec] + [_whole(a) for a in flat] + sh.tri_pieces(),
-                [jax.ShapeDtypeStruct((sh.rows, sh.width, sh.cz), BF16)], [sh.z_spec], [sh.scr_y], **move)
+def finish_project(sh, params, z, m, t, **move):
+    return call(sh, "finish_project", _finish_project_kernel, sh.grid, params, (z, m, t[0]) + (t[1],) * sh.topo.nb,
+                [sh.z_spec, sh.m_spec] + sh.tri_pieces(), [sh.zt, sh.sides], [sh.zt_spec, sh.sides_spec], [sh.scr_y, sh.scr], **move)
+
+
+def finish(sh, params, zt, t, **move):
+    return call(sh, "finish", _finish_kernel, sh.grid, params, (zt, t[0]) + (t[1],) * sh.topo.nb,
+                [sh.zt_spec] + sh.tri_pieces(), [sh.z_out], [sh.z_spec], [sh.scr_y], **move)
+
+
+def finish_last(sh, params, zt, t, other):
+    return call(sh, "finish_last", _finish_last_kernel, sh.grid, params, (zt, other, t[0]) + (t[1],) * sh.topo.nb,
+                [sh.zt_spec, sh.z_spec] + sh.tri_pieces(), [sh.z_out, sh.z_out], [sh.z_spec, sh.z_spec], [sh.scr_y])
 
 
 def triangle(sh, sides, contract, **move):
     nb = sh.topo.nb
-    return call(sh, "triangle", lambda topo, *refs: _triangle_kernel(topo, contract, *refs), (sh.topo.nq,),
+    return call(sh, "triangle", lambda topo, *refs: _triangle_kernel(topo, contract, *refs), (sh.topo.nq,), (),
                 ((sides[0],) + (sides[1],) * nb) * 2, sh.side_pieces(0) + sh.side_pieces(1),
                 [sh.tri], [pl.BlockSpec((1, None) + sh.bits + (sh.rows, sh.width), lambda q: (q,) + (0,) * (nb + 3))],
                 [sh.mat, sh.mat], **move)
-
-
-def _lanes(norm):
-    return jnp.broadcast_to(norm.astype(F32)[..., None], norm.shape + (LANES,))
 
 
 def solution(mesh):
@@ -440,22 +444,19 @@
 
     def per_device(z_one, mask_one, z_two, mask_two, norm_in, w_proj, w_gate, norm_mid, w_out):
         sh = Shapes(n, z_one, w_proj)
-        nin, mid = _lanes(norm_in), _lanes(norm_mid)
-        wp, wg, wo = (jnp.swapaxes(w, 1, 2) for w in (w_proj, w_gate, w_out))
-        zs, ms = (z_one, z_two), (mask_one, mask_two)
-        mask_a, mask_b = ms
-        s1, = project(sh, zs[0], mask_a, nin[0], wp[0])
-        s2, w1 = project(sh, zs[1], mask_b, nin[0], wp[0], moving=s1, cid=0, pace=5.5)
+        first = ((norm_in, 0), (w_proj, 0))
+        middle = ((norm_in, 0), (norm_mid, 0), (w_gate, 0), (w_out, 0), (norm_in, 1), (w_proj, 1))
+        last = ((norm_in, 1), (norm_mid, 1), (w_gate, 1), (w_out, 1))
+        s1, = project(sh, first, z_one, mask_one)
+        s2, w1 = project(sh, first, z_two, mask_two, moving=s1, cid=0, pace=6)
         t1, w2 = triangle(sh, (s1, w1), 1, moving=s2, cid=1)
         t2, v1 = triangle(sh, (s2, w2), 1, moving=t1, cid=2)
-        flat = (nin[0], mid[0], wg[0], wo[0], nin[1], wp[1])
-        zt1, s1, v2 = finish_project(sh, zs[0], mask_a, *flat, (t1, v1), moving=t2, cid=3, pace=1.6)
-        zt2, s2, w1 = finish_project(sh, zs[1], mask_b, *flat, (t2, v2), moving=s1, cid=4, pace=3.2)
+        zt1, s1, v2 = finish_project(sh, middle, z_one, mask_one, (t1, v1), moving=t2, cid=3, pace=1.6)
+        zt2, s2, w1 = finish_project(sh, middle, z_two, mask_two, (t2, v2), moving=s1, cid=4, pace=3.2)
         t1, w2 = triangle(sh, (s1, w1), 0, moving=s2, cid=5)
         t2, v1 = triangle(sh, (s2, w2), 0, moving=t1, cid=6)
-        flat = (nin[1], mid[1], wg[1], wo[1])
-        z1, v2 = finish(sh, zt1, *flat, (t1, v1), moving=t2, cid=7, pace=3.4)
-        z2, = finish(sh, zt2, *flat, (t2, v2))
+        z1, v2 = finish(sh, last, zt1, (t1, v1), moving=t2, cid=7, pace=3.4)
+        z2, z1 = finish_last(sh, last, zt2, (t2, v2), z1)
         return z1, z2
 
     return jax.shard_map(per_device, mesh=mesh,

time: 734 us -> 711 us (0.969)
  local copies, waits for them, and re-layouts: 11.9 us -> 0 us
  Pallas kernels: 720 us -> 709 us
    pallas_call x10, Pallas kernels: 720 us -> 709 us  [call(): pl.pallas_call(kernel, grid=grid, out_shape=tuple(outs), in_specs=in_spec...]
where the time goes in v4:
time: 711 us; the launch traced here: 710 us
  Pallas kernels  709 us (100%)
    pallas_call x10, Pallas kernels, call(): pl.pallas_call(kernel, grid=grid, out_shape=tuple(outs), in_specs=in_spec...  709 us

profile of v4, /device:TPU:97, one launch (start us, length us, event | category | flops | bytes accessed | tf_op | source)
XLA Modules:
  0.0 710.2 jit_solution(14168039710013134278)
XLA Ops:
  0.6 19.4 %project.2.refs_4_.refs_0_.refs_6_ = bf16[4,2,2,2,2,2,2,24,768]{8,7,6,5,4,3,2,1,0:T(8,128)(2,1)} custom-call(bf16[2,2,128]{2,1,0:T(2,128)(2,1)} %refs_0_.11, bf16[2,128,512]{2,1,0:T(8,128)(2,1)} %refs_5_.3, bf16[24,768,128]{2,1,0:T(8,128)(2,1)} %refs_6_.2, s32[24,768]{1,0:T(8,128)} %refs_7_.2), custom_call_target="tpu_custom_call" | custom-call | tf_op jit(solution)/shard_map/project/pallas_call | solution.py:407
  20.1 112.7 %project.3 = (bf16[4,2,2,2,2,2,2,24,768]{8,7,6,5,4,3,2,1,0:T(8,128)(2,1)}, bf16[4,2,5,2,2,2,2,2,24,768]{9,8,7,6,5,4,3,2,1,0:T(8,128)(2,1)}) custom-call(bf16[2,2,128]{2,1,0:T(2,128)(2,1)} %refs_0_.11, bf16[2,128,512]{2,1,0:T(8,128)(2,1)} %refs_5_.3, bf16[24,768,128]{2,1,0:T(8,128)(2,1)} %refs_6_.3, s32[24,768]{1,0:T(8,128)} %refs_7_.3, ...), custom_call_target="tpu_custom_call" | custom-call | tf_op jit(solution)/shard_map/project/pallas_call | solution.py:407
  132.8 107.1 %triangle.4 = (bf16[4,1,2,2,2,2,2,24,768]{8,7,6,5,4,3,2,1,0:T(8,128)(2,1)}, bf16[4,2,5,2,2,2,2,2,24,768]{9,8,7,6,5,4,3,2,1,0:T(8,128)(2,1)}) custom-call(bf16[4,2,2,2,2,2,2,24,768]{8,7,6,5,4,3,2,1,0:T(8,128)(2,1)} %project.2.refs_4_.refs_0_.refs_6_, ...), custom_call_target="tpu_custom_call" | custom-call | tf_op jit(solution)/shard_map/triangle/pallas_call | solution.py:407
  239.9 58.9 %triangle.5 = (bf16[4,1,2,2,2,2,2,24,768]{8,7,6,5,4,3,2,1,0:T(8,128)(2,1)}, bf16[4,1,5,2,2,2,2,2,24,768]{9,8,7,6,5,4,3,2,1,0:T(8,128)(2,1)}) custom-call(bf16[4,2,2,2,2,2,2,24,768]{8,7,6,5,4,3,2,1,0:T(8,128)(2,1)} %get-tuple-element.22.refs_12_.refs_0_.refs_6_, ...), custom_call_target="tpu_custom_call" | custom-call | tf_op jit(solution)/shard_map/triangle/pallas_call | solution.py:407
  298.8 60.4 %finish_project.2 = (bf16[24,128,768]{2,1,0:T(8,128)(2,1)}, bf16[4,2,2,2,2,2,2,24,768]{8,7,6,5,4,3,2,1,0:T(8,128)(2,1)}, bf16[4,1,5,2,2,2,2,2,24,768]{9,8,7,6,5,4,3,2,1,0:T(8,128)(2,1)}) custom-call(bf16[2,2,128]{2,1,0:T(2,128)(2,1)} %refs_0_.11, bf16[2,2,128]{2,1,0:T(2,128)(2,1)} %refs_1_.11, bf16[2,128,128]{2,1,0:T(8,128)(2,1)} %refs_2_.11, ...), custom_call_target="tpu_custom_call" | custom-call | tf_op jit(solution)/shard_map/finish_project/pallas_call | solution.py:407
  359.2 107.4 %finish_project.3 = (bf16[24,128,768]{2,1,0:T(8,128)(2,1)}, bf16[4,2,2,2,2,2,2,24,768]{8,7,6,5,4,3,2,1,0:T(8,128)(2,1)}, bf16[4,2,5,2,2,2,2,2,24,768]{9,8,7,6,5,4,3,2,1,0:T(8,128)(2,1)}) custom-call(bf16[2,2,128]{2,1,0:T(2,128)(2,1)} %refs_0_.11, bf16[2,2,128]{2,1,0:T(2,128)(2,1)} %refs_1_.11, bf16[2,128,128]{2,1,0:T(8,128)(2,1)} %refs_2_.11, ...), custom_call_target="tpu_custom_call" | custom-call | tf_op jit(solution)/shard_map/finish_project/pallas_call | solution.py:407
  466.5 107.9 %triangle.6 = (bf16[4,1,2,2,2,2,2,24,768]{8,7,6,5,4,3,2,1,0:T(8,128)(2,1)}, bf16[4,2,5,2,2,2,2,2,24,768]{9,8,7,6,5,4,3,2,1,0:T(8,128)(2,1)}) custom-call(bf16[4,2,2,2,2,2,2,24,768]{8,7,6,5,4,3,2,1,0:T(8,128)(2,1)} %get-tuple-element.29.refs_14_.refs_0_.refs_6_, ...), custom_call_target="tpu_custom_call" | custom-call | tf_op jit(solution)/shard_map/triangle/pallas_call | solution.py:407
  574.4 58.7 %triangle.7 = (bf16[4,1,2,2,2,2,2,24,768]{8,7,6,5,4,3,2,1,0:T(8,128)(2,1)}, bf16[4,1,5,2,2,2,2,2,24,768]{9,8,7,6,5,4,3,2,1,0:T(8,128)(2,1)}) custom-call(bf16[4,2,2,2,2,2,2,24,768]{8,7,6,5,4,3,2,1,0:T(8,128)(2,1)} %get-tuple-element.33.refs_12_.refs_0_.refs_6_, ...), custom_call_target="tpu_custom_call" | custom-call | tf_op jit(solution)/shard_map/triangle/pallas_call | solution.py:407
  633.1 57.3 %finish.1 = (bf16[24,768,128]{2,1,0:T(8,128)(2,1)}, bf16[4,1,5,2,2,2,2,2,24,768]{9,8,7,6,5,4,3,2,1,0:T(8,128)(2,1)}) custom-call(bf16[2,2,128]{2,1,0:T(2,128)(2,1)} %refs_0_.11, bf16[2,2,128]{2,1,0:T(2,128)(2,1)} %refs_1_.11, bf16[2,128,128]{2,1,0:T(8,128)(2,1)} %refs_2_.11, bf16[2,128,128]{2,1,0:T(8,128)(2,1)} %refs_3_.11, ...), custom_call_target="tpu_custom_call" | custom-call | tf_op jit(solution)/shard_map/finish/pallas_call | solution.py:407
  690.4 19.6 %finish_last.1 = (bf16[24,768,128]{2,1,0:T(8,128)(2,1)}, bf16[24,768,128]{2,1,0:T(8,128)(2,1)}) custom-call(bf16[2,2,128]{2,1,0:T(2,128)(2,1)} %refs_0_.11, bf16[2,2,128]{2,1,0:T(2,128)(2,1)} %refs_1_.11, bf16[2,128,128]{2,1,0:T(8,128)(2,1)} %refs_2_.11, bf16[2,128,128]{2,1,0:T(8,128)(2,1)} %refs_3_.11, bf16[24,128,768]{2,1,0:T(8,128)(2,1)} %get-tuple-element.30.refs_4_, ...), custom_call_target="tpu_custom_call" | custom-call | tf_op jit(solution)/shard_map/finish_last/pallas_call | solution.py:407

commit v5 on v4

--- a/solution.py
+++ b/solution.py
@@ -10,7 +10,7 @@
 
 RB = 8
 LANES = 128
-UNROLL = 4
+PART = 128
 F32, BF16 = jnp.float32, jnp.bfloat16
 
 
@@ -25,12 +25,18 @@
     return lax.dot_general(a, b, (((1,), (0,)), ((), ())), preferred_element_type=F32)
 
 
-def _project(z_t, norm_ref, wp_ref, scr, r, kk):
+def _project(zs, norm_ref, wp_ref, scr, r):
     hid = wp_ref.shape[0] // 4
-    q = _mm(wp_ref[...], _norm_cols(z_t, norm_ref[0], norm_ref[1]))
+    x = jnp.concatenate([_norm_cols(z_t, norm_ref[0], norm_ref[1]) for z_t in zs], axis=1)
+    part = min(PART, hid)
     for s in range(2):
-        p, g = q[2 * s * hid:(2 * s + 1) * hid], q[(2 * s + 1) * hid:(2 * s + 2) * hid]
-        scr[kk, pl.ds(s * hid * RB + r, hid, stride=RB), :] = jax.nn.sigmoid(g) * p
+        for h in range(0, hid, part):
+            p = _mm(wp_ref[2 * s * hid + h:2 * s * hid + h + part], x)
+            g = _mm(wp_ref[(2 * s + 1) * hid + h:(2 * s + 1) * hid + h + part], x)
+            for kk in range(len(zs)):
+                lanes = slice(kk * LANES, (kk + 1) * LANES)
+                v = jax.nn.sigmoid(g[:, lanes]) * p[:, lanes]
+                scr[kk, pl.ds((s * hid + h) * RB + r, part, stride=RB), :] = v
 
 
 def _each_tile(width, f):
@@ -82,13 +88,16 @@
     _each_tile(scr_y.shape[0] * LANES, tile)
 
 
-def _row_loop(width, f):
+def _lanes(width):
+    return [slice(at, at + LANES) for at in range(0, width, LANES)]
+
+
+def _row_loop(f, unroll=RB):
     def body(i, c):
-        for u in range(UNROLL):
-            for kk in range(width // LANES):
-                f(i * UNROLL + u, kk, slice(kk * LANES, (kk + 1) * LANES))
+        for u in range(unroll):
+            f(i * unroll + u)
         return c
-    lax.fori_loop(0, RB // UNROLL, body, 0)
+    lax.fori_loop(0, RB // unroll, body, 0)
 
 
 class Topo:
@@ -236,9 +245,7 @@
 
 
 def _project_kernel(topo, norm, wp, z_ref, m_ref, out_ref, scr):
-    def row(r, kk, lanes):
-        _project(z_ref[r, lanes, :].astype(F32).T, norm, wp, scr, r, kk)
-    _row_loop(z_ref.shape[1], row)
+    _row_loop(lambda r: _project([z_ref[r, lanes, :].T.astype(F32) for lanes in _lanes(z_ref.shape[1])], norm, wp, scr, r))
     _emit_sides(scr, m_ref, out_ref, topo)
 
 
@@ -246,11 +253,14 @@
     t_refs, (zt_ref, out_ref, scr_y, scr) = refs[:-4], refs[-4:]
     _norm_mid(t_refs, scr_y, topo)
 
-    def row(r, kk, lanes):
-        z_new = _finish(z_ref[r, lanes, :].astype(F32).T, r, kk, scr_y, n0, mid, wg, wo)
-        zt_ref[r, :, lanes] = z_new
-        _project(z_new.astype(F32), n1, wp, scr, r, kk)
-    _row_loop(z_ref.shape[1], row)
+    def row(r):
+        news = []
+        for kk, lanes in enumerate(_lanes(z_ref.shape[1])):
+            z_new = _finish(z_ref[r, lanes, :].T.astype(F32), r, kk, scr_y, n0, mid, wg, wo)
+            zt_ref[r, :, lanes] = z_new
+            news.append(z_new.astype(F32))
+        _project(news, n1, wp, scr, r)
+    _row_loop(row, RB // 2)
     _emit_sides(scr, m_ref, out_ref, topo)
 
 
@@ -258,10 +268,11 @@
     t_refs, (z_ref, scr_y) = refs[:-2], refs[-2:]
     _norm_mid(t_refs, scr_y, topo)
 
-    def row(r, kk, lanes):
-        z_new = _finish(zt_ref[r, :, lanes].astype(F32), r, kk, scr_y, n0, mid, wg, wo)
-        z_ref[r, lanes, :] = z_new.astype(F32).T.astype(BF16)
-    _row_loop(z_ref.shape[1], row)
+    def row(r):
+        for kk, lanes in enumerate(_lanes(z_ref.shape[1])):
+            z_new = _finish(zt_ref[r, :, lanes].astype(F32), r, kk, scr_y, n0, mid, wg, wo)
+            z_ref[r, lanes, :] = z_new.T
+    _row_loop(row)
 
 
 def _finish_last_kernel(topo, n0, mid, wg, wo, zt_ref, other_ref, *refs):
@@ -270,31 +281,53 @@
     _finish_kernel(topo, n0, mid, wg, wo, zt_ref, *t_refs, z_ref, scr_y)
 
 
-def _triangle_kernel(topo, contract, *refs):
-    half = (len(refs) - 3) // 2
-    a_refs, b_refs, (out_ref, a_scr, b_scr) = refs[:half], refs[half:2 * half], refs[-3:]
-    n, rows, width = a_scr.shape
+def _triangle_kernel(topo, contract, s_ref, w_ref, out_ref, a_scr, b_scr, t_scr, in_sem, out_sem):
+    n, rows, width = a_scr.shape[1:]
     step = pl.program_id(0)
-
-    def gather(q):
-        for i, (piece, idx, owner) in enumerate(topo.landed(topo.order(q))):
-            a_scr[i] = a_refs[piece][(0,) + idx]
-            b_scr[topo.natural(owner) if contract else i] = b_refs[piece][(0,) + idx]
-
-    def scatter(q):
-        for p in range(n):
-            out_ref[(0,) + topo.relative(topo.order(q), p)] = a_scr[p]
+    slot = lax.rem(step, 2)
+
+    def load(q):
+        for i, (rho, owner) in enumerate(topo.blocks(topo.order(q))):
+            last = max([k for k, f in enumerate(rho) if f], default=-1)
+            for side, scr in enumerate((a_scr, b_scr)):
+                src = s_ref.at[(q, side) + rho] if last < 0 else w_ref.at[(q, side, last) + rho]
+                at = topo.natural(owner) if side and contract else i
+                pltpu.make_async_copy(src, scr.at[q % 2, at], in_sem.at[q % 2, side]).start()
+
+    def store(q):
+        if contract:
+            places = [rho for rho, _ in topo.blocks(topo.order(q))]
+        else:
+            places = [topo.relative(topo.order(q), p) for p in range(n)]
+        for i, place in enumerate(places):
+            pltpu.make_async_copy(t_scr.at[q % 2, i], out_ref.at[(q, 0) + place], out_sem.at[q % 2]).start()
+
+    def wait(scr, at, sem):
+        pltpu.make_async_copy(scr.at[at], scr.at[at], sem).wait()
+
     for q in range(topo.nq):
-        pl.when(step == q)(functools.partial(gather, q))
-    a, b = a_scr[...].reshape(n * rows, width), b_scr[...].reshape(n * rows, width)
+        @pl.when(step == q)
+        def _():
+            if q == 0:
+                load(0)
+            if q + 1 < topo.nq:
+                load(q + 1)
+    wait(a_scr, slot, in_sem.at[slot, 0])
+    wait(b_scr, slot, in_sem.at[slot, 1])
+    a, b = a_scr[slot].reshape(n * rows, width), b_scr[slot].reshape(n * rows, width)
     t = lax.dot_general(a, b, (((contract,), (contract,)), ((), ())), preferred_element_type=F32)
-    t = t.astype(BF16).reshape(n, rows, width)
-    if contract:
-        out_ref[...] = t.reshape(out_ref.shape)
-    else:
-        a_scr[...] = t
-        for q in range(topo.nq):
-            pl.when(step == q)(functools.partial(scatter, q))
+
+    @pl.when(step >= 2)
+    def _():
+        wait(t_scr, slot, out_sem.at[slot])
+    t_scr[slot] = t.astype(BF16).reshape(n, rows, width)
+    for q in range(topo.nq):
+        pl.when(step == q)(functools.partial(store, q))
+
+    @pl.when(step == topo.nq - 1)
+    def _():
+        for k in range(min(2, topo.nq)):
+            wait(t_scr, k, out_sem.at[k])
 
 
 def _whole(a):
@@ -321,7 +354,7 @@
         self.zt = jax.ShapeDtypeStruct((self.rows, self.cz, self.width), BF16)
         self.scr = pltpu.VMEM((self.kb // LANES, 2 * self.hid * RB, LANES), F32)
         self.scr_y = pltpu.VMEM((self.kb // LANES, self.hid * RB, LANES), F32)
-        self.mat = pltpu.VMEM((n, self.rows, self.width), BF16)
+        self.mat = pltpu.VMEM((2, n, self.rows, self.width), BF16)
 
     def landing(self, src):
         return jax.ShapeDtypeStruct(src.shape[:2] + (self.topo.nb,) + src.shape[2:], BF16)
@@ -337,9 +370,6 @@
 
     def tri_pieces(self):
         return self._pieces(self.topo.nq, (RB, self.kb), lambda g: ((0, 0), (g[0], g[1])))
-
-    def side_pieces(self, side):
-        return self._pieces(1, (self.rows, self.width), lambda g: ((g[0], side), (0, 0)))
 
 
 def _prepare(raw, ready, update):
@@ -429,11 +459,10 @@
 
 
 def triangle(sh, sides, contract, **move):
-    nb = sh.topo.nb
+    hbm = pl.BlockSpec(memory_space=pl.ANY)
     return call(sh, "triangle", lambda topo, *refs: _triangle_kernel(topo, contract, *refs), (sh.topo.nq,), (),
-                ((sides[0],) + (sides[1],) * nb) * 2, sh.side_pieces(0) + sh.side_pieces(1),
-                [sh.tri], [pl.BlockSpec((1, None) + sh.bits + (sh.rows, sh.width), lambda q: (q,) + (0,) * (nb + 3))],
-                [sh.mat, sh.mat], **move)
+                sides, [hbm, hbm], [sh.tri], [hbm],
+                [sh.mat, sh.mat, sh.mat, pltpu.SemaphoreType.DMA((2, 2)), pltpu.SemaphoreType.DMA((2,))], **move)
 
 
 def solution(mesh):
@@ -451,7 +480,7 @@
         s2, w1 = project(sh, first, z_two, mask_two, moving=s1, cid=0, pace=6)
         t1, w2 = triangle(sh, (s1, w1), 1, moving=s2, cid=1)
         t2, v1 = triangle(sh, (s2, w2), 1, moving=t1, cid=2)
-        zt1, s1, v2 = finish_project(sh, middle, z_one, mask_one, (t1, v1), moving=t2, cid=3, pace=1.6)
+        zt1, s1, v2 = finish_project(sh, middle, z_one, mask_one, (t1, v1), moving=t2, cid=3, pace=1.3)
         zt2, s2, w1 = finish_project(sh, middle, z_two, mask_two, (t2, v2), moving=s1, cid=4, pace=3.2)
         t1, w2 = triangle(sh, (s1, w1), 0, moving=s2, cid=5)
         t2, v1 = triangle(sh, (s2, w2), 0, moving=t1, cid=6)

time: 711 us -> 694 us (0.976)
  Pallas kernels: 709 us -> 691 us
    pallas_call x10, Pallas kernels: 709 us -> 691 us  [call(): pl.pallas_call(kernel, grid=grid, out_shape=tuple(outs), in_specs=in_spec...]
where the time goes in v5:
time: 694 us; the launch traced here: 692 us
  Pallas kernels  691 us (100%)
    pallas_call x10, Pallas kernels, call(): pl.pallas_call(kernel, grid=grid, out_shape=tuple(outs), in_specs=in_spec...  691 us

profile of v5, /device:TPU:97, one launch (start us, length us, event | category | flops | bytes accessed | tf_op | source)
XLA Modules:
  0.0 692.3 jit_solution(9320382853854730962)
XLA Ops:
  0.6 15.3 %project.2.refs_4_.refs_0_ = bf16[4,2,2,2,2,2,2,24,768]{8,7,6,5,4,3,2,1,0:T(8,128)(2,1)} custom-call(bf16[2,2,128]{2,1,0:T(2,128)(2,1)} %refs_0_.11, bf16[2,128,512]{2,1,0:T(8,128)(2,1)} %refs_5_.3, bf16[24,768,128]{2,1,0:T(8,128)(2,1)} %refs_6_.2, s32[24,768]{1,0:T(8,128)} %refs_7_.2), custom_call_target="tpu_custom_call" | custom-call | tf_op jit(solution)/shard_map/project/pallas_call | solution.py:437
  15.9 112.7 %project.3 = (bf16[4,2,2,2,2,2,2,24,768]{8,7,6,5,4,3,2,1,0:T(8,128)(2,1)}, bf16[4,2,5,2,2,2,2,2,24,768]{9,8,7,6,5,4,3,2,1,0:T(8,128)(2,1)}) custom-call(bf16[2,2,128]{2,1,0:T(2,128)(2,1)} %refs_0_.11, bf16[2,128,512]{2,1,0:T(8,128)(2,1)} %refs_5_.3, bf16[24,768,128]{2,1,0:T(8,128)(2,1)} %refs_6_.3, s32[24,768]{1,0:T(8,128)} %refs_7_.3, ...), custom_call_target="tpu_custom_call" | custom-call | tf_op jit(solution)/shard_map/project/pallas_call | solution.py:437
  128.6 104.5 %triangle.4 = (bf16[4,1,2,2,2,2,2,24,768]{8,7,6,5,4,3,2,1,0:T(8,128)(2,1)}, bf16[4,2,5,2,2,2,2,2,24,768]{9,8,7,6,5,4,3,2,1,0:T(8,128)(2,1)}) custom-call(bf16[4,2,2,2,2,2,2,24,768]{8,7,6,5,4,3,2,1,0:T(8,128)(2,1)} %project.2.refs_4_.refs_0_, bf16[4,2,5,2,2,2,2,2,24,768]{9,8,7,6,5,4,3,2,1,0:T(8,128)(2,1)} %get-tuple-element.23.refs_1_, ...), custom_call_target="tpu_custom_call" | custom-call | tf_op jit(solution)/shard_map/triangle/pallas_call | solution.py:437
  233.1 56.2 %triangle.5 = (bf16[4,1,2,2,2,2,2,24,768]{8,7,6,5,4,3,2,1,0:T(8,128)(2,1)}, bf16[4,1,5,2,2,2,2,2,24,768]{9,8,7,6,5,4,3,2,1,0:T(8,128)(2,1)}) custom-call(bf16[4,2,2,2,2,2,2,24,768]{8,7,6,5,4,3,2,1,0:T(8,128)(2,1)} %get-tuple-element.22.refs_2_.refs_0_, bf16[4,2,5,2,2,2,2,2,24,768]{9,8,7,6,5,4,3,2,1,0:T(8,128)(2,1)} %get-tuple-element.24.refs_1_, ...), custom_call_target="tpu_custom_call" | custom-call | tf_op jit(solution)/shard_map/triangle/pallas_call | solution.py:437
  289.3 58.7 %finish_project.2 = (bf16[24,128,768]{2,1,0:T(8,128)(2,1)}, bf16[4,2,2,2,2,2,2,24,768]{8,7,6,5,4,3,2,1,0:T(8,128)(2,1)}, bf16[4,1,5,2,2,2,2,2,24,768]{9,8,7,6,5,4,3,2,1,0:T(8,128)(2,1)}) custom-call(bf16[2,2,128]{2,1,0:T(2,128)(2,1)} %refs_0_.11, bf16[2,2,128]{2,1,0:T(2,128)(2,1)} %refs_1_.11, bf16[2,128,128]{2,1,0:T(8,128)(2,1)} %refs_2_.11, ...), custom_call_target="tpu_custom_call" | custom-call | tf_op jit(solution)/shard_map/finish_project/pallas_call | solution.py:437
  348.0 107.7 %finish_project.3 = (bf16[24,128,768]{2,1,0:T(8,128)(2,1)}, bf16[4,2,2,2,2,2,2,24,768]{8,7,6,5,4,3,2,1,0:T(8,128)(2,1)}, bf16[4,2,5,2,2,2,2,2,24,768]{9,8,7,6,5,4,3,2,1,0:T(8,128)(2,1)}) custom-call(bf16[2,2,128]{2,1,0:T(2,128)(2,1)} %refs_0_.11, bf16[2,2,128]{2,1,0:T(2,128)(2,1)} %refs_1_.11, bf16[2,128,128]{2,1,0:T(8,128)(2,1)} %refs_2_.11, ...), custom_call_target="tpu_custom_call" | custom-call | tf_op jit(solution)/shard_map/finish_project/pallas_call | solution.py:437
  455.7 104.6 %triangle.6 = (bf16[4,1,2,2,2,2,2,24,768]{8,7,6,5,4,3,2,1,0:T(8,128)(2,1)}, bf16[4,2,5,2,2,2,2,2,24,768]{9,8,7,6,5,4,3,2,1,0:T(8,128)(2,1)}) custom-call(bf16[4,2,2,2,2,2,2,24,768]{8,7,6,5,4,3,2,1,0:T(8,128)(2,1)} %get-tuple-element.29.refs_14_.refs_0_, bf16[4,2,5,2,2,2,2,2,24,768]{9,8,7,6,5,4,3,2,1,0:T(8,128)(2,1)} %get-tuple-element.32.refs_1_, ...), custom_call_target="tpu_custom_call" | custom-call | tf_op jit(solution)/shard_map/triangle/pallas_call | solution.py:437
  560.3 56.2 %triangle.7 = (bf16[4,1,2,2,2,2,2,24,768]{8,7,6,5,4,3,2,1,0:T(8,128)(2,1)}, bf16[4,1,5,2,2,2,2,2,24,768]{9,8,7,6,5,4,3,2,1,0:T(8,128)(2,1)}) custom-call(bf16[4,2,2,2,2,2,2,24,768]{8,7,6,5,4,3,2,1,0:T(8,128)(2,1)} %get-tuple-element.33.refs_2_.refs_0_, bf16[4,2,5,2,2,2,2,2,24,768]{9,8,7,6,5,4,3,2,1,0:T(8,128)(2,1)} %get-tuple-element.35.refs_1_, ...), custom_call_target="tpu_custom_call" | custom-call | tf_op jit(solution)/shard_map/triangle/pallas_call | solution.py:437
  616.5 57.4 %finish.1 = (bf16[24,768,128]{2,1,0:T(8,128)(2,1)}, bf16[4,1,5,2,2,2,2,2,24,768]{9,8,7,6,5,4,3,2,1,0:T(8,128)(2,1)}) custom-call(bf16[2,2,128]{2,1,0:T(2,128)(2,1)} %refs_0_.11, bf16[2,2,128]{2,1,0:T(2,128)(2,1)} %refs_1_.11, bf16[2,128,128]{2,1,0:T(8,128)(2,1)} %refs_2_.11, bf16[2,128,128]{2,1,0:T(8,128)(2,1)} %refs_3_.11, ...), custom_call_target="tpu_custom_call" | custom-call | tf_op jit(solution)/shard_map/finish/pallas_call | solution.py:437
  673.9 18.2 %finish_last.1 = (bf16[24,768,128]{2,1,0:T(8,128)(2,1)}, bf16[24,768,128]{2,1,0:T(8,128)(2,1)}) custom-call(bf16[2,2,128]{2,1,0:T(2,128)(2,1)} %refs_0_.11, bf16[2,2,128]{2,1,0:T(2,128)(2,1)} %refs_1_.11, bf16[2,128,128]{2,1,0:T(8,128)(2,1)} %refs_2_.11, bf16[2,128,128]{2,1,0:T(8,128)(2,1)} %refs_3_.11, bf16[24,128,768]{2,1,0:T(8,128)(2,1)} %get-tuple-element.30.refs_4_, ...), custom_call_target="tpu_custom_call" | custom-call | tf_op jit(solution)/shard_map/finish_last/pallas_call | solution.py:437

commit v6 on v5

--- a/solution.py
+++ b/solution.py
@@ -381,6 +381,16 @@
         ready[...] = raw[update].astype(F32).T.astype(BF16)
 
 
+def _at(ref, spec, grid, g):
+    ids = []
+    for size in grid[::-1]:
+        ids.append(lax.rem(g, size))
+        g = g // size
+    idx = spec.index_map(*ids[::-1])
+    return ref.at[tuple(i if b is None else pl.ds(i * b if isinstance(i, int) else pl.multiple_of(i * b, b), b)
+                        for i, b in zip(idx, spec.block_shape))]
+
+
 def call(sh, name, body, grid, params, ins, in_specs, outs, out_specs, scratch, moving=None, cid=0, pace=None):
     topo = sh.topo
     steps = math.prod(grid)
@@ -396,6 +406,16 @@
         sems = [pltpu.SemaphoreType.DMA((topo.nq, 2, topo.nb))] * 2
         compiler.update(collective_id=cid, has_side_effects=True)
     n_move = len(sems) // 2
+    own_in, own_out = [], []
+    if n_move:
+        own_in = [(k, in_specs[n_par + k]) for k in range(n_in) if in_specs[n_par + k].block_shape is not None]
+        own_out = [(k, out_specs[k]) for k in range(n_out) if out_specs[k].block_shape is not None]
+        in_specs = in_specs[:n_par] + [hbm] * (n_in + 1)
+        out_specs = [hbm] * (n_out + 1)
+        for arrays, own, skip in ((ins, own_in, n_par), (outs, own_out, 0)):
+            scratch += [pltpu.VMEM((2,) + tuple(b for b in spec.block_shape if b is not None), arrays[skip + k].dtype) for k, spec in own]
+        if own_in:
+            sems = [pltpu.SemaphoreType.DMA((2, len(own_in))), pltpu.SemaphoreType.DMA((2, len(own_out)))] + sems
 
     def kernel(*refs):
         topo.here()
@@ -404,7 +424,12 @@
         src, refs = refs[:n_move], refs[n_move:]
         work_out, refs = refs[:n_out], refs[n_out:]
         dst, refs = refs[:n_move], refs[n_move:]
-        done, work_scr, sem_refs = refs[:n_par], refs[n_par:len(refs) - 2 * n_move], refs[len(refs) - 2 * n_move:]
+        refs, sem_refs = refs[:len(refs) - 2 * n_move], refs[len(refs) - 2 * n_move:]
+        if own_in:
+            in_sem, out_sem = refs[-2:]
+            held = refs[-2 - len(own_in) - len(own_out):-2]
+            refs = refs[:-2 - len(own_in) - len(own_out)]
+        done, work_scr = refs[:n_par], refs[n_par:]
         step = pl.program_id(0)
         for d, size in enumerate(grid[1:], 1):
             step = step * size + pl.program_id(d)
@@ -425,7 +450,46 @@
             now = [m for d, m in due if d == g]
             if now:
                 pl.when(step == g)(lambda now=now: [m() for m in now] and None)
-        body(topo, *done, *work_in, *work_out, *work_scr)
+        hand_in, hand_out = list(work_in), list(work_out)
+        if own_in:
+            slot = lax.rem(step, 2)
+
+            def bring(g, i, spec, k):
+                return pltpu.make_async_copy(_at(work_in[k], spec, grid, g), held[i].at[lax.rem(g, 2)], in_sem.at[lax.rem(g, 2), i])
+
+            def take(g, i, spec, k):
+                return pltpu.make_async_copy(held[len(own_in) + i].at[lax.rem(g, 2)], _at(work_out[k], spec, grid, g),
+                                             out_sem.at[lax.rem(g, 2), i])
+
+            @pl.when(step == 0)
+            def _():
+                for i, (k, spec) in enumerate(own_in):
+                    bring(step, i, spec, k).start()
+
+            @pl.when(step + 1 < steps)
+            def _():
+                for i, (k, spec) in enumerate(own_in):
+                    bring(step + 1, i, spec, k).start()
+            for i, (k, spec) in enumerate(own_in):
+                bring(step, i, spec, k).wait()
+                hand_in[k] = held[i].at[slot]
+
+            @pl.when(step >= 2)
+            def _():
+                for i, (k, spec) in enumerate(own_out):
+                    take(step - 2, i, spec, k).wait()
+            for i, (k, spec) in enumerate(own_out):
+                hand_out[k] = held[len(own_in) + i].at[slot]
+        body(topo, *done, *hand_in, *hand_out, *work_scr)
+        if own_in:
+            for i, (k, spec) in enumerate(own_out):
+                take(step, i, spec, k).start()
+
+            @pl.when(step == steps - 1)
+            def _():
+                for g in range(max(0, steps - 2), steps):
+                    for i, (k, spec) in enumerate(own_out):
+                        take(g, i, spec, k).wait()
         if n_move:
             @pl.when(step == steps - 1)
             def _():

time: 694 us -> 689 us (level)
  no operation moved by 1% of the time
where the time goes in v6:
time: 689 us; the launch traced here: 687 us
  Pallas kernels  686 us (100%)
    pallas_call x10, Pallas kernels, call(): pl.pallas_call(kernel, grid=grid, out_shape=tuple(outs), in_specs=in_spec...  686 us

profile of v6, /device:TPU:97, one launch (start us, length us, event | category | flops | bytes accessed | tf_op | source)
XLA Modules:
  0.0 687.3 jit_solution(8194531420342295283)
XLA Ops:
  0.6 15.3 %project.2.refs_4_.refs_0_ = bf16[4,2,2,2,2,2,2,24,768]{8,7,6,5,4,3,2,1,0:T(8,128)(2,1)} custom-call(bf16[2,2,128]{2,1,0:T(2,128)(2,1)} %refs_0_.11, bf16[2,128,512]{2,1,0:T(8,128)(2,1)} %refs_5_.3, bf16[24,768,128]{2,1,0:T(8,128)(2,1)} %refs_6_.2, s32[24,768]{1,0:T(8,128)} %refs_7_.2), custom_call_target="tpu_custom_call" | custom-call | tf_op jit(solution)/shard_map/project/pallas_call | solution.py:501
  15.9 111.5 %project.3 = (bf16[4,2,2,2,2,2,2,24,768]{8,7,6,5,4,3,2,1,0:T(8,128)(2,1)}, bf16[4,2,5,2,2,2,2,2,24,768]{9,8,7,6,5,4,3,2,1,0:T(8,128)(2,1)}) custom-call(bf16[2,2,128]{2,1,0:T(2,128)(2,1)} %refs_0_.11, bf16[2,128,512]{2,1,0:T(8,128)(2,1)} %refs_5_.3, bf16[24,768,128]{2,1,0:T(8,128)(2,1)} %refs_6_.3, s32[24,768]{1,0:T(8,128)} %refs_7_.3, ...), custom_call_target="tpu_custom_call" | custom-call | tf_op jit(solution)/shard_map/project/pallas_call | solution.py:501
  127.4 104.5 %triangle.4 = (bf16[4,1,2,2,2,2,2,24,768]{8,7,6,5,4,3,2,1,0:T(8,128)(2,1)}, bf16[4,2,5,2,2,2,2,2,24,768]{9,8,7,6,5,4,3,2,1,0:T(8,128)(2,1)}) custom-call(bf16[4,2,2,2,2,2,2,24,768]{8,7,6,5,4,3,2,1,0:T(8,128)(2,1)} %project.2.refs_4_.refs_0_, bf16[4,2,5,2,2,2,2,2,24,768]{9,8,7,6,5,4,3,2,1,0:T(8,128)(2,1)} %get-tuple-element.23.refs_1_, ...), custom_call_target="tpu_custom_call" | custom-call | tf_op jit(solution)/shard_map/triangle/pallas_call | solution.py:501
  231.9 56.2 %triangle.5 = (bf16[4,1,2,2,2,2,2,24,768]{8,7,6,5,4,3,2,1,0:T(8,128)(2,1)}, bf16[4,1,5,2,2,2,2,2,24,768]{9,8,7,6,5,4,3,2,1,0:T(8,128)(2,1)}) custom-call(bf16[4,2,2,2,2,2,2,24,768]{8,7,6,5,4,3,2,1,0:T(8,128)(2,1)} %get-tuple-element.22.refs_2_.refs_0_, bf16[4,2,5,2,2,2,2,2,24,768]{9,8,7,6,5,4,3,2,1,0:T(8,128)(2,1)} %get-tuple-element.24.refs_1_, ...), custom_call_target="tpu_custom_call" | custom-call | tf_op jit(solution)/shard_map/triangle/pallas_call | solution.py:501
  288.1 57.3 %finish_project.2 = (bf16[24,128,768]{2,1,0:T(8,128)(2,1)}, bf16[4,2,2,2,2,2,2,24,768]{8,7,6,5,4,3,2,1,0:T(8,128)(2,1)}, bf16[4,1,5,2,2,2,2,2,24,768]{9,8,7,6,5,4,3,2,1,0:T(8,128)(2,1)}) custom-call(bf16[2,2,128]{2,1,0:T(2,128)(2,1)} %refs_0_.11, bf16[2,2,128]{2,1,0:T(2,128)(2,1)} %refs_1_.11, bf16[2,128,128]{2,1,0:T(8,128)(2,1)} %refs_2_.11, ...), custom_call_target="tpu_custom_call" | custom-call | tf_op jit(solution)/shard_map/finish_project/pallas_call | solution.py:501
  345.4 106.3 %finish_project.3 = (bf16[24,128,768]{2,1,0:T(8,128)(2,1)}, bf16[4,2,2,2,2,2,2,24,768]{8,7,6,5,4,3,2,1,0:T(8,128)(2,1)}, bf16[4,2,5,2,2,2,2,2,24,768]{9,8,7,6,5,4,3,2,1,0:T(8,128)(2,1)}) custom-call(bf16[2,2,128]{2,1,0:T(2,128)(2,1)} %refs_0_.11, bf16[2,2,128]{2,1,0:T(2,128)(2,1)} %refs_1_.11, bf16[2,128,128]{2,1,0:T(8,128)(2,1)} %refs_2_.11, ...), custom_call_target="tpu_custom_call" | custom-call | tf_op jit(solution)/shard_map/finish_project/pallas_call | solution.py:501
  451.8 104.5 %triangle.6 = (bf16[4,1,2,2,2,2,2,24,768]{8,7,6,5,4,3,2,1,0:T(8,128)(2,1)}, bf16[4,2,5,2,2,2,2,2,24,768]{9,8,7,6,5,4,3,2,1,0:T(8,128)(2,1)}) custom-call(bf16[4,2,2,2,2,2,2,24,768]{8,7,6,5,4,3,2,1,0:T(8,128)(2,1)} %get-tuple-element.29.refs_14_.refs_0_, bf16[4,2,5,2,2,2,2,2,24,768]{9,8,7,6,5,4,3,2,1,0:T(8,128)(2,1)} %get-tuple-element.32.refs_1_, ...), custom_call_target="tpu_custom_call" | custom-call | tf_op jit(solution)/shard_map/triangle/pallas_call | solution.py:501
  556.3 56.2 %triangle.7 = (bf16[4,1,2,2,2,2,2,24,768]{8,7,6,5,4,3,2,1,0:T(8,128)(2,1)}, bf16[4,1,5,2,2,2,2,2,24,768]{9,8,7,6,5,4,3,2,1,0:T(8,128)(2,1)}) custom-call(bf16[4,2,2,2,2,2,2,24,768]{8,7,6,5,4,3,2,1,0:T(8,128)(2,1)} %get-tuple-element.33.refs_2_.refs_0_, bf16[4,2,5,2,2,2,2,2,24,768]{9,8,7,6,5,4,3,2,1,0:T(8,128)(2,1)} %get-tuple-element.35.refs_1_, ...), custom_call_target="tpu_custom_call" | custom-call | tf_op jit(solution)/shard_map/triangle/pallas_call | solution.py:501
  612.6 56.3 %finish.1 = (bf16[24,768,128]{2,1,0:T(8,128)(2,1)}, bf16[4,1,5,2,2,2,2,2,24,768]{9,8,7,6,5,4,3,2,1,0:T(8,128)(2,1)}) custom-call(bf16[2,2,128]{2,1,0:T(2,128)(2,1)} %refs_0_.11, bf16[2,2,128]{2,1,0:T(2,128)(2,1)} %refs_1_.11, bf16[2,128,128]{2,1,0:T(8,128)(2,1)} %refs_2_.11, bf16[2,128,128]{2,1,0:T(8,128)(2,1)} %refs_3_.11, ...), custom_call_target="tpu_custom_call" | custom-call | tf_op jit(solution)/shard_map/finish/pallas_call | solution.py:501
  668.9 18.2 %finish_last.1 = (bf16[24,768,128]{2,1,0:T(8,128)(2,1)}, bf16[24,768,128]{2,1,0:T(8,128)(2,1)}) custom-call(bf16[2,2,128]{2,1,0:T(2,128)(2,1)} %refs_0_.11, bf16[2,2,128]{2,1,0:T(2,128)(2,1)} %refs_1_.11, bf16[2,128,128]{2,1,0:T(8,128)(2,1)} %refs_2_.11, bf16[2,128,128]{2,1,0:T(8,128)(2,1)} %refs_3_.11, bf16[24,128,768]{2,1,0:T(8,128)(2,1)} %get-tuple-element.30.refs_4_, ...), custom_call_target="tpu_custom_call" | custom-call | tf_op jit(solution)/shard_map/finish_last/pallas_call | solution.py:501
